TPU v7x, 128 devices: a whole 4x4x4 slice. The times are simulated.
128 devices in a mesh: dp: 32 (over x, y, core), group: 4 (over z).
Axes of the slice: x: 4, y: 4, z: 4, core: 2. Of those that a mesh axis runs over, the one named last changes fastest.
Arguments:
- images: bfloat16 [16384, 512], P(('dp', 'group')), may hold values from -1 to 1
- texts: bfloat16 [16384, 512], P(('dp', 'group')), may hold values from -1 to 1
- log_scale: float32 [], replicated, may hold values from 2 to 2.7
Outputs:
- grad_images: bfloat16 [16384, 512], P(('dp', 'group'))
- grad_texts: bfloat16 [16384, 512], P(('dp', 'group'))
- loss: float32 [], replicated
- grad_scale: float32 [], replicated
All inputs are finite; a program needn't handle non-finite values.
Results may differ from a plain program's by a relative error of at most 0.0013.
The roundings to bfloat16 on the way count: a program that leaves them out, or rounds other values in their place, can miss the bound.
Values may be sent and summed in bfloat16 or wider, within the bound.
A program may use at most 128 MiB of HBM per device.

v0:
```python
import functools

import jax
import jax.numpy as jnp
from jax import lax
from jax.experimental import pallas as pl
from jax.experimental.pallas import tpu as pltpu
from jax.sharding import PartitionSpec as P

MESH = pl.DeviceIdType.MESH
NT = (((1,), (1,)), ((), ()))
NN = (((1,), (0,)), ((), ()))
TN = (((0,), (0,)), ((), ()))
F32 = jnp.float32
BLOCK, STAT, GRAD, SCALAR = range(4)
UP, DOWN = range(2)
PIECES = 2


def each(count, step):
    if count <= 8:
        for i in range(count):
            step(i)
    else:
        lax.fori_loop(0, count, lambda i, c: (step(i), c)[1], 0)


def kernel(
    gn, dn, images, texts, log_scale, gi_out, gt_out, loss_out, scale_out,
    img_all, txt_all, logits, weights, row_stat, col_stat, top, acc, row_lse, col_lse,
    gi_send, gi_recv, gt_send, gt_recv, gt_side, sc_group, sc_dp, g_send, g_recv, d_send, d_recv,
    hop_send, sum_send, sum_recv, side_send, pass_send, side_recv,
):
    rows, width = images.shape
    g = lax.axis_index("group")
    d = lax.axis_index("dp")
    wide = 2 * rows if dn % 2 == 0 else rows
    per = wide // rows
    chunks = dn // per

    chip, core = d // per, lax.rem(d, per)
    side = chip * per + (per - 1 - core)
    next_g = (lax.min(g + 1, gn - 1), lax.max(g - 1, 0))

    def c_peer(o):
        return lax.rem(chip + o, chunks)

    def hop(way, k):
        return pltpu.make_async_remote_copy(
            src_ref=img_all.at[at(k)], dst_ref=img_all.at[at(k)],
            send_sem=hop_send.at[way, k], recv_sem=g_recv.at[BLOCK, k],
            device_id={"group": next_g[way]}, device_id_type=MESH)

    def first_hop(way):
        return pltpu.make_async_remote_copy(
            src_ref=images, dst_ref=img_all.at[at(g)],
            send_sem=hop_send.at[way, g], recv_sem=g_recv.at[BLOCK, g],
            device_id={"group": next_g[way]}, device_id_type=MESH)

    def sum_hop(way, k, p):
        piece = pl.ds(p * (rows // PIECES), rows // PIECES)
        return pltpu.make_async_remote_copy(
            src_ref=gi_send.at[k, piece], dst_ref=gi_recv.at[way, k, piece],
            send_sem=sum_send.at[way, k, p], recv_sem=sum_recv.at[way, k, p],
            device_id={"group": next_g[way]}, device_id_type=MESH)

    def pass_on(k):
        return pltpu.make_async_remote_copy(
            src_ref=txt_all.at[at(k)], dst_ref=txt_all.at[at(k)],
            send_sem=pass_send.at[k], recv_sem=d_recv.at[BLOCK, k],
            device_id={"dp": side}, device_id_type=MESH)

    def side_copy(c):
        return pltpu.make_async_remote_copy(
            src_ref=gt_send.at[c * per + (per - 1 - core)], dst_ref=gt_side.at[c],
            send_sem=side_send.at[c], recv_sem=side_recv.at[c],
            device_id={"dp": side}, device_id_type=MESH)

    def g_peer(o):
        return lax.rem(g + o, gn)

    def d_peer(o):
        return lax.rem(d + o, dn)

    def at(k, n=rows):
        return pl.ds(pl.multiple_of(k * n, n), n)

    def g_copy(kind, src, dst, to, slot):
        return pltpu.make_async_remote_copy(
            src_ref=src, dst_ref=dst, send_sem=g_send.at[kind, to], recv_sem=g_recv.at[kind, slot],
            device_id={"group": to}, device_id_type=MESH)

    def d_copy(kind, src, dst, to, slot):
        return pltpu.make_async_remote_copy(
            src_ref=src, dst_ref=dst, send_sem=d_send.at[kind, to], recv_sem=d_recv.at[kind, slot],
            device_id={"dp": to}, device_id_type=MESH)

    barrier = pltpu.get_barrier_semaphore()
    each(gn - 1, lambda i: pl.semaphore_signal(
        barrier, inc=1, device_id={"group": g_peer(i + 1)}, device_id_type=MESH))
    each(dn - 1, lambda i: pl.semaphore_signal(
        barrier, inc=1, device_id={"dp": d_peer(i + 1)}, device_id_type=MESH))
    pl.semaphore_wait(barrier, gn + dn - 2)

    def text_block(k):
        return d_copy(BLOCK, texts, txt_all.at[at(d)], k, d)

    @pl.when(g < gn - 1)
    def _():
        first_hop(UP).start()

    @pl.when(g > 0)
    def _():
        first_hop(DOWN).start()

    each(chunks - 1, lambda i: text_block(c_peer(i + 1) * per + core).start())
    if per == 2:
        text_block(side).start()
    img_all[at(g), :] = images[...]
    txt_all[at(d), :] = texts[...]
    s = jnp.exp(log_scale[...])
    eye = (lax.broadcasted_iota(jnp.int32, (rows, rows), 0)
           == lax.broadcasted_iota(jnp.int32, (rows, rows), 1))

    def relay_images(j):
        @pl.when(g - j >= 0)
        def _():
            hop(UP, g - j).wait_recv()

            @pl.when(g < gn - 1)
            def _():
                hop(UP, g - j).start()

        @pl.when(g + j < gn)
        def _():
            hop(DOWN, g + j).wait_recv()

            @pl.when(g > 0)
            def _():
                hop(DOWN, g + j).start()

    def relay_text(i):
        k = c_peer(i + 1) * per + core
        d_copy(BLOCK, texts, txt_all.at[at(k)], k, k).wait_recv()
        if per == 2:
            pass_on(k).start()

    for j in range(1, gn):
        relay_images(j)
        if j == 1:
            each(chunks - 1, relay_text)
    if gn == 1:
        each(chunks - 1, relay_text)

    def logits_chunk(i):
        c = c_peer(i)
        if per == 2:
            k = c * per + (per - 1 - core)
            d_copy(BLOCK, texts, txt_all.at[at(k)], k, k).wait_recv()
        part = s * lax.dot_general(img_all[...], txt_all[at(c, wide), :], NT, preferred_element_type=F32)
        logits[:, at(c, wide)] = part
        high = jnp.max(part, axis=0, keepdims=True)
        col_stat[d, 0:1, at(c, wide)] = high
        col_stat[d, 1:2, at(c, wide)] = jnp.sum(jnp.exp(part - high), axis=0, keepdims=True)
        if isinstance(i, int) and i == 0:
            top[...] = part
        else:
            top[...] = jnp.maximum(top[...], part)

    if chunks > 8:
        top[...] = jnp.full(top.shape, -jnp.inf, F32)
    each(chunks, logits_chunk)
    each(dn - 1, lambda i: d_copy(STAT, col_stat.at[d], col_stat.at[d], d_peer(i + 1), d).start())

    def flat(col):
        return jnp.sum(jnp.where(eye, col, 0.0), axis=0, keepdims=True)

    def stand(line):
        return jnp.sum(jnp.where(eye, line, 0.0), axis=1, keepdims=True)

    for k in range(gn):
        band = pl.ds(k * rows, rows)
        high = jnp.max(top[band, :], axis=1, keepdims=True)
        acc[...] = jnp.zeros(acc.shape, F32)

        def add(c):
            acc[...] += jnp.exp(logits[band, at(c, wide)] - high)

        each(chunks, add)
        row_stat[g, 0:1, band] = flat(high)
        row_stat[g, 1:2, band] = flat(jnp.sum(acc[...], axis=1, keepdims=True))
    each(gn - 1, lambda i: g_copy(STAT, row_stat.at[g], row_stat.at[g], g_peer(i + 1), g).start())

    def wait_row(i):
        k = g_peer(i + 1)
        g_copy(STAT, row_stat.at[k], row_stat.at[k], k, k).wait_recv()

    def wait_col(i):
        k = d_peer(i + 1)
        d_copy(STAT, col_stat.at[k], col_stat.at[k], k, k).wait_recv()

    def lse(stat):
        high = jnp.max(stat[:, 0, :], axis=0, keepdims=True)
        return high + jnp.log(jnp.sum(stat[:, 1, :] * jnp.exp(stat[:, 0, :] - high), axis=0, keepdims=True))

    each(dn - 1, wait_col)
    col_lse[...] = lse(col_stat)
    each(gn - 1, wait_row)
    row_lse[...] = lse(row_stat)

    acc[...] = jnp.zeros(acc.shape, F32)
    across = 4 * dn * rows
    step_of = (lax.broadcasted_iota(jnp.int32, (rows, wide), 1)
               - lax.broadcasted_iota(jnp.int32, (rows, wide), 0))
    order = sorted(range(gn), key=lambda t: (-abs(2 * t - gn + 1), -t))
    for k in order:
        line = stand(row_lse[0:1, at(k)])

        def weigh(c):
            part = logits[at(k), at(c, wide)]
            w = 0.5 * (jnp.exp(part - line) + jnp.exp(part - col_lse[0:1, at(c, wide)]))
            w = w - jnp.where(step_of == jnp.where(k == g, d * rows - c * wide, -across), 1.0, 0.0)
            acc[...] += w * part
            weights[at(k), at(c, wide)] = w.astype(jnp.bfloat16)

        each(chunks, weigh)
        gi_send[k] = lax.dot_general(weights[at(k), :], txt_all[...], NN, preferred_element_type=F32)
        for p in range(PIECES):
            if k > 0:
                @pl.when(g == 0)
                def _():
                    sum_hop(UP, k, p).start()
            if k < gn - 1:
                @pl.when(g == gn - 1)
                def _():
                    sum_hop(DOWN, k, p).start()

    own = logits[at(g), at(d)]
    pairs = jnp.sum(jnp.where(eye, own, 0.0), axis=0, keepdims=True)
    loss_part = jnp.sum(row_lse[0:1, at(g)] + col_lse[0:1, at(d)] - 2.0 * pairs, axis=1, keepdims=True)
    scale_part = jnp.sum(jnp.sum(acc[...], axis=0, keepdims=True), axis=1, keepdims=True)
    first = lax.broadcasted_iota(jnp.int32, (8, 128), 1) == 0
    sc_group[g] = jnp.where(first, loss_part, scale_part)
    each(gn - 1, lambda i: g_copy(SCALAR, sc_group.at[g], sc_group.at[g], g_peer(i + 1), g).start())

    def share(i):
        c = c_peer(1 + i)
        k = c * per + core
        if per == 2:
            side_copy(c).wait_recv()
            gt_send[k] += gt_side[c]

        @pl.when(c != chip)
        def _():
            pltpu.make_async_remote_copy(
                src_ref=gt_send.at[k], dst_ref=gt_recv.at[chip],
                send_sem=d_send.at[GRAD, c], recv_sem=d_recv.at[GRAD, chip],
                device_id={"dp": k}, device_id_type=MESH).start()

    def text_chunk(i):
        c = c_peer(1 + i)
        part = lax.dot_general(weights[:, at(c, wide)], img_all[...], TN, preferred_element_type=F32)
        for j in range(per):
            gt_send[c * per + j] = part[j * rows:(j + 1) * rows]
        if per == 2:
            side_copy(c).start()
        if isinstance(i, int):
            if i > 0:
                share(i - 1)
        else:
            @pl.when(i > 0)
            def _():
                share(i - 1)

    each(chunks, text_chunk)
    share(chunks - 1)

    def add_sum(way, k, p):
        piece = pl.ds(p * (rows // PIECES), rows // PIECES)
        sum_hop(way, k, p).wait_recv()
        gi_send[k, piece] += gi_recv[way, k, piece]

    for j in range(gn - 1):
        for p in range(PIECES):
            @pl.when((g > 0) & (gn - 1 - j > g))
            def _():
                add_sum(UP, gn - 1 - j, p)
                sum_hop(UP, gn - 1 - j, p).start()

            @pl.when((g < gn - 1) & (j < g))
            def _():
                add_sum(DOWN, j, p)
                sum_hop(DOWN, j, p).start()

    def wait_sc_group(i):
        k = g_peer(i + 1)
        g_copy(SCALAR, sc_group.at[k], sc_group.at[k], k, k).wait_recv()

    each(gn - 1, wait_sc_group)
    sc_dp[d] = jnp.sum(sc_group[...], axis=0)
    each(dn - 1, lambda i: d_copy(SCALAR, sc_dp.at[d], sc_dp.at[d], d_peer(i + 1), d).start())

    def take_d(i):
        c = c_peer(i + 1)
        pltpu.make_async_remote_copy(
            src_ref=gt_recv.at[c], dst_ref=gt_recv.at[c],
            send_sem=d_send.at[GRAD, c], recv_sem=d_recv.at[GRAD, c],
            device_id={"dp": c * per + core}, device_id_type=MESH).wait_recv()
        gt_send[d] += gt_recv[c]

    each(chunks - 1, take_d)
    gt_out[...] = (s * gt_send[d]).astype(gt_out.dtype)

    for p in range(PIECES):
        @pl.when(g > 0)
        def _():
            add_sum(UP, g, p)

        @pl.when(g < gn - 1)
        def _():
            add_sum(DOWN, g, p)

    gi_out[...] = (s * gi_send[g]).astype(gi_out.dtype)

    def wait_sc_dp(i):
        k = d_peer(i + 1)
        d_copy(SCALAR, sc_dp.at[k], sc_dp.at[k], k, k).wait_recv()

    each(dn - 1, wait_sc_dp)
    total = jnp.sum(sc_dp[...], axis=0)
    pair_total = gn * dn * rows
    loss_out[...] = total[0:1, 0:1] / (2.0 * pair_total)
    scale_out[...] = total[0:1, 1:2] / pair_total

    def end_g(i):
        k = g_peer(i + 1)
        g_copy(STAT, row_stat.at[g], row_stat.at[g], k, g).wait_send()
        g_copy(SCALAR, sc_group.at[g], sc_group.at[g], k, g).wait_send()

    def end_d(i):
        k = d_peer(i + 1)
        d_copy(STAT, col_stat.at[d], col_stat.at[d], k, d).wait_send()
        d_copy(SCALAR, sc_dp.at[d], sc_dp.at[d], k, d).wait_send()

    def end_c(i):
        c = c_peer(i + 1)
        k = c * per + core
        text_block(k).wait_send()
        if per == 2:
            pass_on(k).wait_send()
            side_copy(c).wait_send()
        pltpu.make_async_remote_copy(
            src_ref=gt_send.at[k], dst_ref=gt_recv.at[chip],
            send_sem=d_send.at[GRAD, c], recv_sem=d_recv.at[GRAD, chip],
            device_id={"dp": k}, device_id_type=MESH).wait_send()

    each(gn - 1, end_g)
    each(dn - 1, end_d)
    each(chunks - 1, end_c)
    if per == 2:
        text_block(side).wait_send()
        side_copy(chip).wait_send()

    for k in range(gn):
        @pl.when((g < gn - 1) & (k <= g))
        def _():
            hop(UP, k).wait_send()

        @pl.when((g > 0) & (k >= g))
        def _():
            hop(DOWN, k).wait_send()

        for p in range(PIECES):
            @pl.when(k > g)
            def _():
                sum_hop(UP, k, p).wait_send()

            @pl.when(k < g)
            def _():
                sum_hop(DOWN, k, p).wait_send()


def body(gn, dn, images, texts, log_scale):
    rows, width = images.shape
    high, across = gn * rows, dn * rows
    wide = 2 * rows if dn % 2 == 0 else rows
    chunks = across // wide
    vmem = pl.BlockSpec(memory_space=pltpu.VMEM)
    gi, gt, loss, scale = pl.pallas_call(
        functools.partial(kernel, gn, dn),
        out_shape=(
            jax.ShapeDtypeStruct(images.shape, images.dtype),
            jax.ShapeDtypeStruct(texts.shape, texts.dtype),
            jax.ShapeDtypeStruct((1, 1), F32),
            jax.ShapeDtypeStruct((1, 1), F32),
        ),
        in_specs=[vmem] * 3,
        out_specs=(vmem,) * 4,
        scratch_shapes=[
            pltpu.VMEM((high, width), images.dtype),
            pltpu.VMEM((across, width), texts.dtype),
            pltpu.VMEM((high, across), F32),
            pltpu.VMEM((high, across), jnp.bfloat16),
            pltpu.VMEM((gn, 2, high), F32),
            pltpu.VMEM((dn, 2, across), F32),
            pltpu.VMEM((high, wide), F32),
            pltpu.VMEM((rows, wide), F32),
            pltpu.VMEM((1, high), F32),
            pltpu.VMEM((1, across), F32),
            pltpu.VMEM((gn, rows, width), F32),
            pltpu.VMEM((2, gn, rows, width), F32),
            pltpu.VMEM((dn, rows, width), F32),
            pltpu.VMEM((chunks, rows, width), F32),
            pltpu.VMEM((chunks, rows, width), F32),
            pltpu.VMEM((gn, 8, 128), F32),
            pltpu.VMEM((dn, 8, 128), F32),
            pltpu.SemaphoreType.DMA((4, gn)),
            pltpu.SemaphoreType.DMA((4, gn)),
            pltpu.SemaphoreType.DMA((4, dn)),
            pltpu.SemaphoreType.DMA((4, dn)),
            pltpu.SemaphoreType.DMA((2, gn)),
            pltpu.SemaphoreType.DMA((2, gn, PIECES)),
            pltpu.SemaphoreType.DMA((2, gn, PIECES)),
            pltpu.SemaphoreType.DMA((chunks,)),
            pltpu.SemaphoreType.DMA((dn,)),
            pltpu.SemaphoreType.DMA((chunks,)),
        ],
        compiler_params=pltpu.CompilerParams(
            collective_id=0, has_side_effects=True, vmem_limit_bytes=60 * 1024 * 1024),
    )(images, texts, log_scale.reshape(1, 1))
    return gi, gt, loss.reshape(()), scale.reshape(())


def solution(mesh):
    gn, dn = mesh.shape["group"], mesh.shape["dp"]
    spec = P(("dp", "group"), None)
    return jax.shard_map(
        functools.partial(body, gn, dn), mesh=mesh, in_specs=(spec, spec, P()),
        out_specs=(spec, spec, P(), P()), check_vma=False)
```

profile of v0, /device:TPU:5, one launch (start us, length us, event | category | flops | bytes accessed | tf_op | source)
XLA Modules:
  0.0 177.3 jit_solution(811541500465387571)
XLA Ops:
  1.3 170.2 %shard_map.66 = (bf16[128,512]{1,0:T(8,128)(2,1)}, bf16[128,512]{1,0:T(8,128)(2,1)}, f32[1,1]{1,0:T(1,128)}, f32[1,1]{1,0:T(1,128)}) custom-call(bf16[128,512]{1,0:T(8,128)(2,1)} %images.1, bf16[128,512]{1,0:T(8,128)(2,1)} %texts.1, f32[1,1]{1,0:T(1,128)} %bitcast.3.log_scale), custom_call_target="tpu_custom_call" | custom-call | tf_op jit(solution)/shard_map/pallas_call | solution.py:389
  171.5 0.0 copy-start
  171.5 1.6 copy.12
  173.1 0.0 copy-done
  173.1 0.7 copy.13
Async XLA Ops:
  171.5 1.6 copy-start
where the time goes:
time: 177 us
  Pallas kernels  170 us (96%)
  between operations  4.78 us (3%)
  local copies, waits for them, and re-layouts  2.26 us (1%)
    pallas_call x1, Pallas kernels, body(): pl.pallas_call(functools.partial(kernel, gn, dn), out_shape=(jax.ShapeDty...  170 us

commit v1 on v0

v1 whole, which is shorter than its diff:
```python
import functools
import math

import jax
import jax.numpy as jnp
from jax import lax
from jax.experimental import pallas as pl
from jax.experimental.pallas import tpu as pltpu
from jax.sharding import PartitionSpec as P

MESH = pl.DeviceIdType.MESH
NT = (((1,), (1,)), ((), ()))
NN = (((1,), (0,)), ((), ()))
F32 = jnp.float32
BF16 = jnp.bfloat16
LOG2E = math.log2(math.e)
LN2 = math.log(2.0)

SLOTS = ((0, 0), (1, 0), (0, 1), (0, 3), (1, 1), (1, 3), (0, 2), (1, 2))
INDEX = {slot: j for j, slot in enumerate(SLOTS)}
RING = 4
COUNT = len(SLOTS)
IMG, TXT = 0, 1
CUT = 2
FLIP, UP, DOWN, FLIP_UP, FLIP_DOWN, FAR, FLIP_FAR = range(7)
R5, R4, R3A, R3B, R2A, R2B, R1 = range(7)


def back(j):
    f, o = SLOTS[j]
    return INDEX[f, (RING - o) % RING]


def seen(j, k):
    f, o = SLOTS[j]
    a, b = SLOTS[k]
    return INDEX[f ^ a, (o - b) % RING]


def kernel(
    images, texts, log_scale, gi_out, gt_out, loss_out, scale_out,
    img, img_t, txt, logits, weights, row_top, row_sum, col_top, col_sum, row_all, col_all, row_lse, col_lse,
    gi, gi_far, gi_pair, gi_recv, gt, gt_recv, sc_one, sc_two, sc_three,
    a_send, a_recv, c_send, c_recv, st_send, st_recv, ct_send, ct_recv,
    r_send, r_recv, p_send, p_recv, s1_send, s1_recv, s2_send, s2_recv, s3_send, s3_recv,
):
    rows, width = images.shape
    pair = 2 * rows
    z = lax.axis_index("group")
    d = lax.axis_index("dp")
    core = lax.rem(d, 2)
    y = lax.rem(lax.div(d, 2), RING)
    x = lax.div(d, 2 * RING)
    mate = 1 - core
    ahead = 1 + 2 * core
    behind = 3 - 2 * core
    slot_n = 2 + core
    slot_r = 3 - core

    def dp_of(a, b, c):
        return (a * RING + b) * 2 + c

    x_img = x + 1 - 2 * lax.rem(x, 2)
    x_txt = 3 - x

    def img_dev(f, o, k):
        return {"dp": dp_of(x_img if f else x, y, mate if k else core), "group": lax.rem(z + o, RING)}

    def txt_dev(f, o):
        return {"dp": dp_of(x_txt if f else x, lax.rem(y + o, RING), core), "group": z}

    def dev(stream, f, o):
        return img_dev(f, o, 0) if stream == IMG else txt_dev(f, o)

    def rcopy(src, dst, send, recv, to):
        return pltpu.make_async_remote_copy(
            src_ref=src, dst_ref=dst, send_sem=send, recv_sem=recv, device_id=to, device_id_type=MESH)

    def all_img_peers():
        return [(j, k) for j in range(COUNT) for k in range(2) if (j, k) != (0, 0)]

    barrier = pltpu.get_barrier_semaphore()
    for j, k in all_img_peers():
        pl.semaphore_signal(barrier, inc=1, device_id=img_dev(*SLOTS[j], k), device_id_type=MESH)
    for j in range(1, COUNT):
        pl.semaphore_signal(barrier, inc=1, device_id=txt_dev(*SLOTS[j]), device_id_type=MESH)
    pl.semaphore_wait(barrier, 2 * COUNT - 1 + COUNT - 1)

    cut = rows // CUT

    def at(n, size):
        return pl.ds(n, size) if isinstance(n, int) else pl.ds(pl.multiple_of(n, 16), size)

    def place(stream, j, h):
        return img.at[at(j * pair + h * cut, cut)] if stream == IMG else txt.at[at(j * rows + h * cut, cut)]

    def a_copy(stream, kind, h):
        own = (images if stream == IMG else texts).at[pl.ds(h * cut, cut)]
        src, j, to = {
            FLIP: (own, 1, (1, 0)),
            UP: (own, 3, (0, 1)),
            DOWN: (own, 2, (0, 3)),
            FLIP_UP: (place(stream, 1, h), 5, (0, 1)),
            FLIP_DOWN: (place(stream, 1, h), 4, (0, 3)),
            FAR: (place(stream, slot_r, h), 6, (0, ahead)),
            FLIP_FAR: (place(stream, 6, h), 7, (1, 0)),
        }[kind]
        return rcopy(src, place(stream, j, h), a_send.at[stream, kind, h], a_recv.at[stream, j, h], dev(stream, *to))

    def a_wait(stream, j, h):
        ref = place(stream, j, h)
        rcopy(ref, ref, a_send.at[stream, FLIP, h], a_recv.at[stream, j, h], dev(stream, 1, 0)).wait_recv()

    def c_copy(j, h):
        src = images.at[pl.ds(h * cut, cut)] if isinstance(j, int) and j == 0 else place(IMG, j, h)
        return rcopy(src, img.at[at(j * pair + rows + h * cut, cut)], c_send.at[j, h], c_recv.at[j, h], img_dev(0, 0, 1))

    for h in range(CUT):
        for kind in (FLIP, UP, DOWN):
            for stream in (IMG, TXT):
                a_copy(stream, kind, h).start()
    for h in range(CUT):
        c_copy(0, h).start()
    img[0:rows, :] = images[...]
    txt[0:rows, :] = texts[...]
    s = jnp.exp(log_scale[...])
    s2 = s * LOG2E

    def arrive(stream, j, h):
        a_wait(stream, j, h)
        if stream == IMG:
            c_copy(j, h).start()

    for h in range(CUT):
        for stream in (IMG, TXT):
            arrive(stream, 1, h)
            a_copy(stream, FLIP_UP, h).start()
            a_copy(stream, FLIP_DOWN, h).start()
        for stream in (IMG, TXT):
            arrive(stream, slot_r, h)
            a_copy(stream, FAR, h).start()
            arrive(stream, slot_n, h)

    def region(i, n, c0, cols, fresh_row, fresh_col):
        rr = pl.ds(i * pair, n * pair) if isinstance(i, int) else pl.ds(pl.multiple_of(i * pair, pair), n * pair)
        part = s2 * lax.dot_general(img[rr, :], txt[pl.ds(c0, cols), :], NT, preferred_element_type=F32)
        logits[rr, pl.ds(c0, cols)] = part
        high = functools.reduce(jnp.maximum, [part[:, t:t + 128] for t in range(0, cols, 128)])
        if not fresh_row:
            old = row_top[rr, :]
            high = jnp.maximum(high, old)
        total = functools.reduce(jnp.add, [jnp.exp2(part[:, t:t + 128] - high) for t in range(0, cols, 128)])
        if not fresh_row:
            total += row_sum[rr, :] * jnp.exp2(old - high)
        row_top[rr, :] = high
        row_sum[rr, :] = total
        tall = part.reshape(n * pair // 8, 8, cols)
        high = jnp.max(tall, axis=0)
        cc = pl.ds(c0, cols)
        old = col_top[:, cc]
        high = jnp.maximum(high, old)
        col_sum[:, cc] = (col_sum[:, cc] * jnp.exp2(old - high)
                          + jnp.sum(jnp.exp2(tall - high[None]), axis=0))
        col_top[:, cc] = high

    def loop(lo, hi, step):
        lax.fori_loop(lo, hi, lambda i, c: (step(i), c)[1], 0)

    def pair_in(j):
        for h in range(CUT):
            c_copy(j, h).wait_recv()

    def turn(j):
        img_t[:, pl.ds(j * pair, pair)] = img[pl.ds(j * pair, pair), :].T

    col_top[...] = jnp.full(col_top.shape, -1e30, F32)
    col_sum[...] = jnp.zeros(col_sum.shape, F32)
    for j in range(4):
        pair_in(j)
    loop(0, 4, lambda i: region(i, 1, 0, 4 * rows, True, True))
    for h in range(CUT):
        for stream in (IMG, TXT):
            arrive(stream, 6, h)
            a_copy(stream, FLIP_FAR, h).start()
    for h in range(CUT):
        for stream in (IMG, TXT):
            arrive(stream, 4, h)
            arrive(stream, 5, h)
    for j in range(4):
        turn(j)
    for j in (4, 5, 6):
        pair_in(j)
    loop(0, 2, lambda i: region(2 * i, 2, 4 * rows, 2 * rows, False, True))
    loop(4, 7, lambda i: region(i, 1, 0, 6 * rows, True, False))
    for j in (4, 5, 6):
        turn(j)
    for h in range(CUT):
        for stream in (TXT, IMG):
            arrive(stream, 7, h)
    loop(0, 7, lambda i: region(i, 1, 6 * rows, 2 * rows, False, False))
    pair_in(7)
    region(7, 1, 0, 8 * rows, True, False)
    turn(7)

    eye = (lax.broadcasted_iota(jnp.int32, (rows, rows), 0)
           == lax.broadcasted_iota(jnp.int32, (rows, rows), 1))

    def close_row(b):
        rr = pl.ds(b * rows, rows) if isinstance(b, int) else pl.ds(pl.multiple_of(b * rows, rows), rows)
        top = row_top[rr, :]
        high = jnp.max(top, axis=1, keepdims=True)
        total = jnp.sum(row_sum[rr, :] * jnp.exp2(top - high), axis=1, keepdims=True)
        lse = high + jnp.log(total) * LOG2E
        row_all[0, b] = jnp.sum(jnp.where(eye, lse, 0.0), axis=0, keepdims=True)

    for b in range(2 * COUNT):
        close_row(b)
    high = jnp.max(col_top[...], axis=0, keepdims=True)
    lse = high + jnp.log(jnp.sum(col_sum[...] * jnp.exp2(col_top[...] - high), axis=0, keepdims=True)) * LOG2E
    for j in range(COUNT):
        col_all[0, j] = lse[:, j * rows:(j + 1) * rows]

    def row_copy(j, k):
        return rcopy(row_all.at[0], row_all.at[back(j) * 2 + k], st_send.at[j * 2 + k],
                     st_recv.at[back(j) * 2 + k], img_dev(*SLOTS[j], k))

    def col_copy(j):
        return rcopy(col_all.at[0], col_all.at[back(j)], ct_send.at[j], ct_recv.at[back(j)], txt_dev(*SLOTS[j]))

    for j in reversed(range(COUNT)):
        for k in (1, 0):
            if (j, k) != (0, 0):
                row_copy(j, k).start()
        if j:
            col_copy(j).start()

    def join(values):
        high = functools.reduce(jnp.maximum, values)
        total = functools.reduce(jnp.add, [jnp.exp2(v - high) for v in values])
        return high + jnp.log(total) * LOG2E

    for j in range(1, COUNT):
        rcopy(col_all.at[j], col_all.at[j], ct_send.at[j], ct_recv.at[j], txt_dev(1, 0)).wait_recv()
    for j in range(COUNT):
        col_lse[0:1, j * rows:(j + 1) * rows] = join([col_all[k, seen(j, k)] for k in range(COUNT)])
    for j, k in all_img_peers():
        n = j * 2 + k
        rcopy(row_all.at[n], row_all.at[n], st_send.at[n], st_recv.at[n], img_dev(1, 0, 0)).wait_recv()
    own_row = None
    for j in range(COUNT):
        for k in range(2):
            line = join([row_all[a * 2 + b, seen(j, a) * 2 + (k ^ b)] for a in range(COUNT) for b in range(2)])
            if (j, k) == (0, 0):
                own_row = line
            row_lse[pl.ds((j * 2 + k) * rows, rows), :] = jnp.broadcast_to(line, (rows, rows)).T

    own = logits[0:rows, 0:rows]
    own_pairs = jnp.sum(jnp.where(eye, own, 0.0), axis=0, keepdims=True)
    loss_part = LN2 * jnp.sum(own_row + col_lse[0:1, 0:rows] - 2.0 * own_pairs, axis=1, keepdims=True)

    def weigh(i, acc):
        rr = pl.ds(pl.multiple_of(i * pair, pair), pair)
        line = row_lse[rr, :] + 1.0
        for t in range(0, COUNT * rows, rows):
            part = logits[rr, t:t + rows]
            w = jnp.exp2(part - line) + jnp.exp2(part - (col_lse[0:1, t:t + rows] + 1.0))
            weights[rr, t:t + rows] = w.astype(BF16)
            acc += jnp.sum((w * part).reshape(pair // 8, 8, rows), axis=0)
        return acc

    acc = lax.fori_loop(0, COUNT, weigh, jnp.zeros((8, rows), F32))
    w = jnp.exp2(own - (row_lse[0:rows, :] + 1.0)) + jnp.exp2(own - (col_lse[0:1, 0:rows] + 1.0))
    weights[0:rows, 0:rows] = (w - jnp.where(eye, 1.0, 0.0)).astype(BF16)
    scale_part = LN2 * jnp.sum(jnp.sum(acc, axis=0, keepdims=True) - own_pairs, axis=1, keepdims=True)
    first = lax.broadcasted_iota(jnp.int32, (1, rows), 1) == 0

    me_one = (lax.rem(x, 2) * RING + z) * 2 + core
    half = lax.div(x, 2)
    sc_one[me_one] = jnp.where(first, loss_part, scale_part)

    def one_copy(j, k):
        return rcopy(sc_one.at[me_one], sc_one.at[me_one], s1_send.at[j * 2 + k], s1_recv.at[me_one],
                     img_dev(*SLOTS[j], k))

    def one_wait(j, k):
        f, o = SLOTS[j]
        xi = lax.rem(x, 2)
        n = ((1 - xi if f else xi) * RING + lax.rem(z + o, RING)) * 2 + (mate if k else core)
        rcopy(sc_one.at[n], sc_one.at[n], s1_send.at[j * 2 + k], s1_recv.at[n], img_dev(*SLOTS[j], k)).wait_recv()

    def two_copy(o):
        return rcopy(sc_two.at[y], sc_two.at[y], s2_send.at[o], s2_recv.at[y], txt_dev(0, o))

    def two_wait(o):
        n = lax.rem(y + o, RING)
        rcopy(sc_two.at[n], sc_two.at[n], s2_send.at[o], s2_recv.at[n], txt_dev(0, o)).wait_recv()

    def three_copy():
        return rcopy(sc_three.at[half], sc_three.at[half], s3_send, s3_recv, txt_dev(1, 0))

    for j, k in all_img_peers():
        one_copy(j, k).start()

    def scalar_two():
        for j, k in all_img_peers():
            one_wait(j, k)
        sc_two[y] = jnp.sum(sc_one[...], axis=0)
        for o in range(1, RING):
            two_copy(o).start()

    def scalar_three():
        for o in range(1, RING):
            two_wait(o)
        sc_three[half] = jnp.sum(sc_two[...], axis=0)
        three_copy().start()

    def gi_block(j):
        part = lax.dot_general(weights[pl.ds(j * pair, pair), :], txt[...], NN, preferred_element_type=F32)
        gi[j] = part[0:rows]
        gi_far[j] = part[rows:pair]
        p_copy(j).start()

    def p_copy(j):
        return rcopy(gi_far.at[j], gi_pair.at[j], p_send.at[j], p_recv.at[j], img_dev(0, 0, 1))

    def pair_sum(j):
        p_copy(j).wait_recv()
        gi[j] += gi_pair[j]

    def gt_block(j):
        part = lax.dot_general(img_t[...], weights[:, pl.ds(j * rows, 2 * rows)], NN, preferred_element_type=F32)
        gt[j] = part[:, 0:rows]
        gt[j + 1] = part[:, rows:2 * rows]

    def piece(stream, ref, j, h):
        n = ref.shape[1] // CUT
        return ref.at[j, pl.ds(h * n, n)]

    def bufs(stream):
        return (gi, gi_recv) if stream == IMG else (gt, gt_recv)

    def r_copy(stream, kind, h):
        src, dst = bufs(stream)
        j, m, to = {
            R5: (7, R5, (1, 0)),
            R4: (6, R4, (0, behind)),
            R3A: (4, R3B, (0, 1)),
            R3B: (5, R3A, (0, 3)),
            R2A: (slot_n, R2A, (0, ahead)),
            R2B: (slot_r, R2B, (0, behind)),
            R1: (1, R1, (1, 0)),
        }[kind]
        return rcopy(piece(stream, src, j, h), piece(stream, dst, m, h), r_send.at[stream, kind, h],
                     r_recv.at[stream, m, h], dev(stream, *to))

    def r_wait(stream, m, h):
        ref = piece(stream, bufs(stream)[1], m, h)
        rcopy(ref, ref, r_send.at[stream, m, h], r_recv.at[stream, m, h], dev(stream, 1, 0)).wait_recv()

    def r_start(stream, kind):
        for h in range(CUT):
            r_copy(stream, kind, h).start()

    def r_add(stream, kind, j, kinds):
        src, dst = bufs(stream)
        n = src.shape[1] // CUT
        for h in range(CUT):
            for m in kinds:
                r_wait(stream, m, h)
            hh = pl.ds(h * n, n)
            total = src[j, hh]
            for m in kinds:
                total += dst[m, hh]
            src[j, hh] = total
            r_copy(stream, kind, h).start()

    gi_block(7)
    gt_block(6)
    r_start(TXT, R5)
    pair_sum(7)
    r_start(IMG, R5)
    gi_block(4)
    gi_block(5)
    gt_block(4)
    r_start(TXT, R3A)
    r_start(TXT, R3B)
    pair_sum(4)
    r_start(IMG, R3A)
    pair_sum(5)
    r_start(IMG, R3B)
    gi_block(6)
    gi_block(1)
    scalar_two()
    gt_block(2)
    r_start(TXT, R2A)
    pair_sum(6)
    r_add(TXT, R4, 6, (R5,))
    r_add(IMG, R4, 6, (R5,))
    gt_block(0)
    gi_block(2)
    gi_block(3)
    pair_sum(2)
    pair_sum(3)
    r_start(IMG, R2A)
    gi_block(0)
    pair_sum(1)
    scalar_three()
    r_add(TXT, R1, 1, (R3A, R3B))
    r_add(IMG, R1, 1, (R3A, R3B))
    r_add(TXT, R2B, slot_r, (R4,))
    r_add(IMG, R2B, slot_r, (R4,))
    pair_sum(0)

    def finish(stream):
        src, dst = bufs(stream)
        for m in (R2A, R1, R2B):
            for h in range(CUT):
                r_wait(stream, m, h)
        return s * (src[0] + dst[R2A] + dst[R1] + dst[R2B])

    gt_out[...] = finish(TXT).T.astype(gt_out.dtype)
    gi_out[...] = finish(IMG).astype(gi_out.dtype)
    other = 1 - half
    rcopy(sc_three.at[other], sc_three.at[other], s3_send, s3_recv, txt_dev(1, 0)).wait_recv()
    total = sc_three[0] + sc_three[1]
    pair_total = 2 * RING * RING * RING * rows
    loss_out[...] = total[0:1, 0:1] / (2.0 * pair_total)
    scale_out[...] = total[0:1, 1:2] / pair_total

    for stream in (IMG, TXT):
        for kind in range(7):
            for h in range(CUT):
                a_copy(stream, kind, h).wait_send()
                r_copy(stream, kind, h).wait_send()
    for j in range(COUNT):
        for h in range(CUT):
            c_copy(j, h).wait_send()
        p_copy(j).wait_send()
        if j:
            col_copy(j).wait_send()
    for j, k in all_img_peers():
        row_copy(j, k).wait_send()
        one_copy(j, k).wait_send()
    for o in range(1, RING):
        two_copy(o).wait_send()
    three_copy().wait_send()


def body(images, texts, log_scale):
    rows, width = images.shape
    vmem = pl.BlockSpec(memory_space=pltpu.VMEM)
    dma = pltpu.SemaphoreType.DMA
    gi, gt, loss, scale = pl.pallas_call(
        kernel,
        out_shape=(
            jax.ShapeDtypeStruct(images.shape, images.dtype),
            jax.ShapeDtypeStruct(texts.shape, texts.dtype),
            jax.ShapeDtypeStruct((1, 1), F32),
            jax.ShapeDtypeStruct((1, 1), F32),
        ),
        in_specs=[vmem] * 3,
        out_specs=(vmem,) * 4,
        scratch_shapes=[
            pltpu.VMEM((2 * COUNT * rows, width), BF16),
            pltpu.VMEM((width, 2 * COUNT * rows), BF16),
            pltpu.VMEM((COUNT * rows, width), BF16),
            pltpu.VMEM((2 * COUNT * rows, COUNT * rows), F32),
            pltpu.VMEM((2 * COUNT * rows, COUNT * rows), BF16),
            pltpu.VMEM((2 * COUNT * rows, rows), F32),
            pltpu.VMEM((2 * COUNT * rows, rows), F32),
            pltpu.VMEM((8, COUNT * rows), F32),
            pltpu.VMEM((8, COUNT * rows), F32),
            pltpu.VMEM((2 * COUNT, 2 * COUNT, 1, rows), F32),
            pltpu.VMEM((COUNT, COUNT, 1, rows), F32),
            pltpu.VMEM((2 * COUNT * rows, rows), F32),
            pltpu.VMEM((1, COUNT * rows), F32),
            pltpu.VMEM((COUNT, rows, width), F32),
            pltpu.VMEM((COUNT, rows, width), F32),
            pltpu.VMEM((COUNT, rows, width), F32),
            pltpu.VMEM((7, rows, width), F32),
            pltpu.VMEM((COUNT, width, rows), F32),
            pltpu.VMEM((7, width, rows), F32),
            pltpu.VMEM((2 * COUNT, 1, rows), F32),
            pltpu.VMEM((RING, 1, rows), F32),
            pltpu.VMEM((2, 1, rows), F32),
            dma((2, 7, CUT)), dma((2, COUNT, CUT)),
            dma((COUNT, CUT)), dma((COUNT, CUT)),
            dma((2 * COUNT,)), dma((2 * COUNT,)),
            dma((COUNT,)), dma((COUNT,)),
            dma((2, 7, CUT)), dma((2, 7, CUT)),
            dma((COUNT,)), dma((COUNT,)),
            dma((2 * COUNT,)), dma((2 * COUNT,)),
            dma((RING,)), dma((RING,)),
            dma, dma,
        ],
        compiler_params=pltpu.CompilerParams(
            collective_id=0, has_side_effects=True, vmem_limit_bytes=60 * 1024 * 1024),
    )(images, texts, log_scale.reshape(1, 1))
    return gi, gt, loss.reshape(()), scale.reshape(())


def solution(mesh):
    spec = P(("dp", "group"), None)
    return jax.shard_map(
        body, mesh=mesh, in_specs=(spec, spec, P()),
        out_specs=(spec, spec, P(), P()), check_vma=False)
```

time: 177 us -> 68.1 us (0.38)
  the two profiles are of different devices: /device:TPU:5 before, /device:TPU:1 now
where the time goes in v1:
time: 68.1 us; the launch traced here: 68 us
  Pallas kernels  60.9 us (89%)
  between operations  4.78 us (7%)
  local copies, waits for them, and re-layouts  2.26 us (3%)
    pallas_call x1, Pallas kernels, body(): pl.pallas_call(kernel, out_shape=(jax.ShapeDtypeStruct(images.shape, imag...  60.9 us
    unnamed x4, local copies, waits for them, and re-layouts  2.26 us

profile of v1, /device:TPU:1, one launch (start us, length us, event | category | flops | bytes accessed | tf_op | source)
XLA Modules:
  0.0 68.0 jit_solution(7055275535204312555)
XLA Ops:
  1.3 60.9 %shard_map.66 = (bf16[128,512]{1,0:T(8,128)(2,1)}, bf16[128,512]{1,0:T(8,128)(2,1)}, f32[1,1]{1,0:T(1,128)}, f32[1,1]{1,0:T(1,128)}) custom-call(bf16[128,512]{1,0:T(8,128)(2,1)} %images.1, bf16[128,512]{1,0:T(8,128)(2,1)} %texts.1, f32[1,1]{1,0:T(1,128)} %bitcast.3.log_scale), custom_call_target="tpu_custom_call" | custom-call | tf_op jit(solution)/shard_map/pallas_call | solution.py:453
  62.2 0.0 copy-start
  62.2 1.6 %copy.12 = bf16[128,512]{1,0:T(8,128)(2,1)} copy(bf16[128,512]{1,0:T(8,128)(2,1)} %get-tuple-element.16) | data formatting | bytes 262144
  63.8 0.0 copy-done
  63.8 0.7 copy.13
Async XLA Ops:
  62.2 1.6 %copy-start = (bf16[128,512]{1,0:T(8,128)(2,1)S(1)}, bf16[128,512]{1,0:T(8,128)(2,1)}, u32[]{:S(2)}) copy-start(bf16[128,512]{1,0:T(8,128)(2,1)} %get-tuple-element.17) | copy-start | bytes 393220

commit v2 on v1

v2 whole, which is shorter than its diff:
```python
import functools
import math

import jax
import jax.numpy as jnp
from jax import lax
from jax.experimental import pallas as pl
from jax.experimental.pallas import tpu as pltpu
from jax.sharding import PartitionSpec as P

MESH = pl.DeviceIdType.MESH
NT = (((1,), (1,)), ((), ()))
NN = (((1,), (0,)), ((), ()))
F32 = jnp.float32
BF16 = jnp.bfloat16
LOG2E = math.log2(math.e)
LN2 = math.log(2.0)

SLOTS = ((0, 0), (1, 0), (0, 1), (0, 3), (1, 1), (1, 3), (0, 2), (1, 2))
INDEX = {slot: j for j, slot in enumerate(SLOTS)}
RING = 4
COUNT = len(SLOTS)
IMG, TXT = 0, 1
CUT = 4
PART = 2
DEPTH = 120.0
FLIP, UP, DOWN, FLIP_UP, FLIP_DOWN, FAR, FLIP_FAR = range(7)


def back(j):
    f, o = SLOTS[j]
    return INDEX[f, (RING - o) % RING]


def seen(j, k):
    f, o = SLOTS[j]
    a, b = SLOTS[k]
    return INDEX[f ^ a, (o - b) % RING]


def kernel(
    images, texts, log_scale, gi_out, gt_out, loss_out, scale_out,
    img, img_t, txt, logits, weights, row_top, row_sum, col_top, col_sum, row_all, col_all, row_lse, col_lse,
    acc, gi, gi_far, gi_pair, gi_code, gi_top, gi_recv, gi_top_recv,
    gt, gt_code, gt_top, gt_recv, gt_top_recv, sc_one, sc_two, sc_three,
    a_send, a_recv, c_send, c_recv, st_send, st_recv, ct_send, ct_recv,
    r_send, r_recv, p_send, p_recv, s1_send, s1_recv, s2_send, s2_recv, s3_send, s3_recv,
):
    rows, width = images.shape
    pair = 2 * rows
    z = lax.axis_index("group")
    d = lax.axis_index("dp")
    core = lax.rem(d, 2)
    y = lax.rem(lax.div(d, 2), RING)
    x = lax.div(d, 2 * RING)
    mate = 1 - core

    def dp_of(a, b, c):
        return (a * RING + b) * 2 + c

    x_img = x + 1 - 2 * lax.rem(x, 2)
    x_txt = 3 - x

    def img_dev(f, o, k):
        return {"dp": dp_of(x_img if f else x, y, mate if k else core), "group": lax.rem(z + o, RING)}

    def txt_dev(f, o):
        return {"dp": dp_of(x_txt if f else x, lax.rem(y + o, RING), core), "group": z}

    def dev(stream, f, o):
        return img_dev(f, o, 0) if stream == IMG else txt_dev(f, o)

    def rcopy(src, dst, send, recv, to):
        return pltpu.make_async_remote_copy(
            src_ref=src, dst_ref=dst, send_sem=send, recv_sem=recv, device_id=to, device_id_type=MESH)

    def all_img_peers():
        return [(j, k) for j in range(COUNT) for k in range(2) if (j, k) != (0, 0)]

    barrier = pltpu.get_barrier_semaphore()
    for j, k in all_img_peers():
        pl.semaphore_signal(barrier, inc=1, device_id=img_dev(*SLOTS[j], k), device_id_type=MESH)
    for j in range(1, COUNT):
        pl.semaphore_signal(barrier, inc=1, device_id=txt_dev(*SLOTS[j]), device_id_type=MESH)
    pl.semaphore_wait(barrier, 2 * COUNT - 1 + COUNT - 1)

    cut = rows // CUT

    def at(n, size):
        return pl.ds(n, size)

    def place(stream, j, h):
        return img.at[at(j * pair + h * cut, cut)] if stream == IMG else txt.at[at(j * rows + h * cut, cut)]

    def a_copy(stream, kind, h):
        own = (images if stream == IMG else texts).at[pl.ds(h * cut, cut)]
        src, j, to = {
            FLIP: (own, 1, (1, 0)),
            UP: (own, 3, (0, 1)),
            DOWN: (own, 2, (0, 3)),
            FLIP_UP: (place(stream, 1, h), 5, (0, 1)),
            FLIP_DOWN: (place(stream, 1, h), 4, (0, 3)),
            FAR: (own, 6, (0, 2)),
            FLIP_FAR: (place(stream, 6, h), 7, (1, 0)),
        }[kind]
        return rcopy(src, place(stream, j, h), a_send.at[stream, kind, h], a_recv.at[stream, j, h], dev(stream, *to))

    def a_wait(stream, j, h):
        ref = place(stream, j, h)
        rcopy(ref, ref, a_send.at[stream, FLIP, h], a_recv.at[stream, j, h], dev(stream, 1, 0)).wait_recv()

    def c_copy(j, h):
        src = images.at[pl.ds(h * cut, cut)] if j == 0 else place(IMG, j, h)
        return rcopy(src, img.at[at(j * pair + rows + h * cut, cut)], c_send.at[j, h], c_recv.at[j, h], img_dev(0, 0, 1))

    for kinds in ((FLIP, FAR), (UP, DOWN)):
        for h in range(CUT):
            for kind in kinds:
                for stream in (IMG, TXT):
                    a_copy(stream, kind, h).start()
    for h in range(CUT):
        c_copy(0, h).start()
    img[0:rows, :] = images[...]
    txt[0:rows, :] = texts[...]
    s = jnp.exp(log_scale[...])
    s2 = s * LOG2E

    def arrive(stream, j, h):
        a_wait(stream, j, h)
        if stream == IMG:
            c_copy(j, h).start()

    for h in range(CUT):
        for stream in (IMG, TXT):
            arrive(stream, 1, h)
            a_copy(stream, FLIP_UP, h).start()
            a_copy(stream, FLIP_DOWN, h).start()
        for stream in (IMG, TXT):
            arrive(stream, 6, h)
            a_copy(stream, FLIP_FAR, h).start()
    for h in range(CUT):
        for stream in (IMG, TXT):
            arrive(stream, 2, h)
            arrive(stream, 3, h)

    span = 4 * rows
    eye = (lax.broadcasted_iota(jnp.int32, (rows, rows), 0)
           == lax.broadcasted_iota(jnp.int32, (rows, rows), 1))

    def product(i, h):
        rr, cc = pl.ds(i * pair, pair), pl.ds(h * span, span)
        logits[rr, cc] = s2 * lax.dot_general(img[rr, :], txt[cc, :], NT, preferred_element_type=F32)

    def stats(i, h):
        rr, cc = pl.ds(i * pair, pair), pl.ds(h * span, span)
        part = logits[rr, cc]
        tiles = [part[:, t:t + rows] for t in range(0, span, rows)]
        high = functools.reduce(jnp.maximum, tiles)
        if h:
            old = row_top[rr, :]
            high = jnp.maximum(high, old)
        total = functools.reduce(jnp.add, [jnp.exp2(t - high) for t in tiles])
        if h:
            total += row_sum[rr, :] * jnp.exp2(old - high)
        row_top[rr, :] = high
        row_sum[rr, :] = total
        tall = part.reshape(pair // 8, 8, span)
        high = jnp.max(tall, axis=0)
        if i:
            old = col_top[:, cc]
            high = jnp.maximum(high, old)
        total = jnp.sum(jnp.exp2(tall - high[None]), axis=0)
        if i:
            total += col_sum[:, cc] * jnp.exp2(old - high)
        col_sum[:, cc] = total
        col_top[:, cc] = high

    def close_row(i):
        for b in (2 * i, 2 * i + 1):
            rr = pl.ds(b * rows, rows)
            top = row_top[rr, :]
            high = jnp.max(top, axis=1, keepdims=True)
            total = jnp.sum(row_sum[rr, :] * jnp.exp2(top - high), axis=1, keepdims=True)
            lse = high + jnp.log(total) * LOG2E
            row_all[0, b] = jnp.sum(jnp.where(eye, lse, 0.0), axis=0, keepdims=True)

    def units(work, close):
        product(*work[0])
        for n, unit in enumerate(work):
            if n + 1 < len(work):
                product(*work[n + 1])
            stats(*unit)
            if close and unit[1]:
                close_row(unit[0])

    def pair_in(j):
        for h in range(CUT):
            c_copy(j, h).wait_recv()

    def turn(j):
        img_t[:, pl.ds(j * pair, pair)] = img[pl.ds(j * pair, pair), :].T

    for j in range(4):
        pair_in(j)
    units([(0, 0), (1, 0), (2, 0), (3, 0)], False)
    for h in range(CUT):
        for stream in (IMG, TXT):
            arrive(stream, 4, h)
            arrive(stream, 5, h)
    for j in (4, 5, 6):
        pair_in(j)
    units([(4, 0), (5, 0), (6, 0)], False)
    for h in range(CUT):
        for stream in (TXT, IMG):
            arrive(stream, 7, h)
    pair_in(7)
    units([(0, 1), (1, 1), (2, 1), (3, 1), (4, 1), (5, 1), (6, 1), (7, 0), (7, 1)], True)

    high = jnp.max(col_top[...], axis=0, keepdims=True)
    lse = high + jnp.log(jnp.sum(col_sum[...] * jnp.exp2(col_top[...] - high), axis=0, keepdims=True)) * LOG2E
    for j in range(COUNT):
        col_all[0, j] = lse[:, j * rows:(j + 1) * rows]

    def row_copy(j, k):
        return rcopy(row_all.at[0], row_all.at[back(j) * 2 + k], st_send.at[j * 2 + k],
                     st_recv.at[back(j) * 2 + k], img_dev(*SLOTS[j], k))

    def col_copy(j):
        return rcopy(col_all.at[0], col_all.at[back(j)], ct_send.at[j], ct_recv.at[back(j)], txt_dev(*SLOTS[j]))

    for j in reversed(range(COUNT)):
        for k in (1, 0):
            if (j, k) != (0, 0):
                row_copy(j, k).start()
        if j:
            col_copy(j).start()

    for j in range(COUNT):
        turn(j)

    def join(values):
        high = functools.reduce(jnp.maximum, values)
        total = functools.reduce(jnp.add, [jnp.exp2(v - high) for v in values])
        return high + jnp.log(total) * LOG2E

    for j in range(1, COUNT):
        rcopy(col_all.at[j], col_all.at[j], ct_send.at[j], ct_recv.at[j], txt_dev(1, 0)).wait_recv()
    for j in range(COUNT):
        col_lse[0:1, j * rows:(j + 1) * rows] = join([col_all[k, seen(j, k)] for k in range(COUNT)])
    for j, k in all_img_peers():
        n = j * 2 + k
        rcopy(row_all.at[n], row_all.at[n], st_send.at[n], st_recv.at[n], img_dev(1, 0, 0)).wait_recv()
    own_row = None
    for j in range(COUNT):
        for k in range(2):
            line = join([row_all[a * 2 + b, seen(j, a) * 2 + (k ^ b)] for a in range(COUNT) for b in range(2)])
            if (j, k) == (0, 0):
                own_row = line
            row_lse[pl.ds((j * 2 + k) * rows, rows), :] = jnp.broadcast_to(line, (rows, rows)).T

    own = logits[0:rows, 0:rows]
    own_pairs = jnp.sum(jnp.where(eye, own, 0.0), axis=0, keepdims=True)
    loss_part = LN2 * jnp.sum(own_row + col_lse[0:1, 0:rows] - 2.0 * own_pairs, axis=1, keepdims=True)

    def weigh(i):
        rr = pl.ds(i * pair, pair)
        line = row_lse[rr, :] + 1.0
        gain = jnp.zeros((8, rows), F32)
        for t in range(0, COUNT * rows, rows):
            part = logits[rr, t:t + rows]
            w = jnp.exp2(part - line) + jnp.exp2(part - (col_lse[0:1, t:t + rows] + 1.0))
            weights[rr, t:t + rows] = w.astype(BF16)
            gain += jnp.sum((w * part).reshape(pair // 8, 8, rows), axis=0)
        acc[i] = gain

    def weigh_own():
        w = jnp.exp2(own - (row_lse[0:rows, :] + 1.0)) + jnp.exp2(own - (col_lse[0:1, 0:rows] + 1.0))
        weights[0:rows, 0:rows] = (w - jnp.where(eye, 1.0, 0.0)).astype(BF16)

    me_one = (lax.rem(x, 2) * RING + z) * 2 + core
    half = lax.div(x, 2)
    first = lax.broadcasted_iota(jnp.int32, (1, rows), 1) == 0

    def one_copy(j, k):
        return rcopy(sc_one.at[me_one], sc_one.at[me_one], s1_send.at[j * 2 + k], s1_recv.at[me_one],
                     img_dev(*SLOTS[j], k))

    def one_wait(j, k):
        f, o = SLOTS[j]
        xi = lax.rem(x, 2)
        n = ((1 - xi if f else xi) * RING + lax.rem(z + o, RING)) * 2 + (mate if k else core)
        rcopy(sc_one.at[n], sc_one.at[n], s1_send.at[j * 2 + k], s1_recv.at[n], img_dev(*SLOTS[j], k)).wait_recv()

    def two_copy(o):
        return rcopy(sc_two.at[y], sc_two.at[y], s2_send.at[o], s2_recv.at[y], txt_dev(0, o))

    def two_wait(o):
        n = lax.rem(y + o, RING)
        rcopy(sc_two.at[n], sc_two.at[n], s2_send.at[o], s2_recv.at[n], txt_dev(0, o)).wait_recv()

    def three_copy():
        return rcopy(sc_three.at[half], sc_three.at[half], s3_send, s3_recv, txt_dev(1, 0))

    def scalar_one():
        gain = jnp.sum(jnp.sum(acc[...], axis=0), axis=0, keepdims=True)
        scale_part = LN2 * jnp.sum(gain - own_pairs, axis=1, keepdims=True)
        sc_one[me_one] = jnp.where(first, loss_part, scale_part)
        for j, k in all_img_peers():
            one_copy(j, k).start()

    def scalar_two():
        for j, k in all_img_peers():
            one_wait(j, k)
        sc_two[y] = jnp.sum(sc_one[...], axis=0)
        for o in range(1, RING):
            two_copy(o).start()

    def scalar_three():
        for o in range(1, RING):
            two_wait(o)
        sc_three[half] = jnp.sum(sc_two[...], axis=0)
        three_copy().start()

    def gi_blocks(j):
        part = lax.dot_general(weights[pl.ds(j * pair, 2 * pair), :], txt[...], NN, preferred_element_type=F32)
        for k in range(2):
            gi[j + k] = part[k * pair:k * pair + rows]
            gi_far[j + k] = part[k * pair + rows:(k + 1) * pair]
            p_copy(j + k).start()

    def p_copy(j):
        return rcopy(gi_far.at[j], gi_pair.at[j], p_send.at[j], p_recv.at[j], img_dev(0, 0, 1))

    def pair_sum(j):
        p_copy(j).wait_recv()
        gi[j] += gi_pair[j]

    def gt_half(h):
        part = lax.dot_general(img_t[...], weights[:, pl.ds(h * span, span)], NN, preferred_element_type=F32)
        for j in range(4):
            gt[4 * h + j] = part[:, j * rows:(j + 1) * rows]

    sums = (gi, gt)
    codes = (gi_code, gt_code)
    tops = (gi_top, gt_top)
    code_in = (gi_recv, gt_recv)
    top_in = (gi_top_recv, gt_top_recv)
    target = {7: (1, 0), 4: (0, 1), 5: (0, 3), 2: (0, 1), 3: (0, 3), 6: (0, 2), 1: (1, 0)}

    def part_of(stream, h):
        n = sums[stream].shape[1] // PART
        return pl.ds(h * n, n)

    def r_copies(stream, j, h):
        hh = part_of(stream, h)
        return [rcopy(src, dst, r_send.at[stream, j, h, k], r_recv.at[stream, j, h, k], dev(stream, *target[j]))
                for k, (src, dst) in enumerate((
                    (codes[stream].at[j, hh], code_in[stream].at[j, hh]),
                    (tops[stream].at[j, h], top_in[stream].at[j, h])))]

    def give(stream, j, h, total):
        top = jnp.maximum(jnp.max(jnp.abs(total), axis=0, keepdims=True), 1e-30)
        codes[stream][j, part_of(stream, h)] = jnp.exp2(total * (DEPTH / top)).astype(BF16)
        tops[stream][j, h] = top * (LOG2E / DEPTH)
        for copy in r_copies(stream, j, h):
            copy.start()

    def take(stream, j, h):
        for copy in r_copies(stream, j, h):
            copy.wait_recv()
        return jnp.log(code_in[stream][j, part_of(stream, h)].astype(F32)) * top_in[stream][j, h]

    def send(stream, *slots):
        for j in slots:
            for h in range(PART):
                give(stream, j, h, sums[stream][j, part_of(stream, h)])

    def send_on(stream, j, sources):
        for h in range(PART):
            total = sums[stream][j, part_of(stream, h)]
            for k in sources:
                total += take(stream, k, h)
            give(stream, j, h, total)

    for j in range(COUNT):
        weigh(j)
    weigh_own()
    scalar_one()
    gt_half(1)
    send(TXT, 7, 4, 5)
    gi_blocks(6)
    gi_blocks(4)
    pair_sum(7)
    send(IMG, 7)
    pair_sum(4)
    send(IMG, 4)
    pair_sum(5)
    send(IMG, 5)
    gt_half(0)
    send(TXT, 2, 3)
    gi_blocks(2)
    gi_blocks(0)
    pair_sum(2)
    send(IMG, 2)
    pair_sum(3)
    send(IMG, 3)
    send_on(TXT, 6, (7,))
    pair_sum(6)
    send_on(IMG, 6, (7,))
    scalar_two()
    send_on(TXT, 1, (4, 5))
    pair_sum(1)
    send_on(IMG, 1, (4, 5))
    scalar_three()
    pair_sum(0)

    def finish(stream):
        out = []
        for h in range(PART):
            total = sums[stream][0, part_of(stream, h)]
            for j in (2, 3, 6, 1):
                total += take(stream, j, h)
            out.append(s * total)
        return jnp.concatenate(out, axis=0)

    gt_out[...] = finish(TXT).T.astype(gt_out.dtype)
    gi_out[...] = finish(IMG).astype(gi_out.dtype)
    other = 1 - half
    rcopy(sc_three.at[other], sc_three.at[other], s3_send, s3_recv, txt_dev(1, 0)).wait_recv()
    total = sc_three[0] + sc_three[1]
    pair_total = 2 * RING * RING * RING * rows
    loss_out[...] = total[0:1, 0:1] / (2.0 * pair_total)
    scale_out[...] = total[0:1, 1:2] / pair_total

    for stream in (IMG, TXT):
        for kind in range(7):
            for h in range(CUT):
                a_copy(stream, kind, h).wait_send()
            for h in range(PART):
                for copy in r_copies(stream, kind + 1, h):
                    copy.wait_send()
    for j in range(COUNT):
        for h in range(CUT):
            c_copy(j, h).wait_send()
        p_copy(j).wait_send()
        if j:
            col_copy(j).wait_send()
    for j, k in all_img_peers():
        row_copy(j, k).wait_send()
        one_copy(j, k).wait_send()
    for o in range(1, RING):
        two_copy(o).wait_send()
    three_copy().wait_send()


def body(images, texts, log_scale):
    rows, width = images.shape
    vmem = pl.BlockSpec(memory_space=pltpu.VMEM)
    dma = pltpu.SemaphoreType.DMA
    gi, gt, loss, scale = pl.pallas_call(
        kernel,
        out_shape=(
            jax.ShapeDtypeStruct(images.shape, images.dtype),
            jax.ShapeDtypeStruct(texts.shape, texts.dtype),
            jax.ShapeDtypeStruct((1, 1), F32),
            jax.ShapeDtypeStruct((1, 1), F32),
        ),
        in_specs=[vmem] * 3,
        out_specs=(vmem,) * 4,
        scratch_shapes=[
            pltpu.VMEM((2 * COUNT * rows, width), BF16),
            pltpu.VMEM((width, 2 * COUNT * rows), BF16),
            pltpu.VMEM((COUNT * rows, width), BF16),
            pltpu.VMEM((2 * COUNT * rows, COUNT * rows), F32),
            pltpu.VMEM((2 * COUNT * rows, COUNT * rows), BF16),
            pltpu.VMEM((2 * COUNT * rows, rows), F32),
            pltpu.VMEM((2 * COUNT * rows, rows), F32),
            pltpu.VMEM((8, COUNT * rows), F32),
            pltpu.VMEM((8, COUNT * rows), F32),
            pltpu.VMEM((2 * COUNT, 2 * COUNT, 1, rows), F32),
            pltpu.VMEM((COUNT, COUNT, 1, rows), F32),
            pltpu.VMEM((2 * COUNT * rows, rows), F32),
            pltpu.VMEM((1, COUNT * rows), F32),
            pltpu.VMEM((COUNT, 8, rows), F32),
            pltpu.VMEM((COUNT, rows, width), F32),
            pltpu.VMEM((COUNT, rows, width), F32),
            pltpu.VMEM((COUNT, rows, width), F32),
            pltpu.VMEM((COUNT, rows, width), BF16),
            pltpu.VMEM((COUNT, PART, 1, width), F32),
            pltpu.VMEM((COUNT, rows, width), BF16),
            pltpu.VMEM((COUNT, PART, 1, width), F32),
            pltpu.VMEM((COUNT, width, rows), F32),
            pltpu.VMEM((COUNT, width, rows), BF16),
            pltpu.VMEM((COUNT, PART, 1, rows), F32),
            pltpu.VMEM((COUNT, width, rows), BF16),
            pltpu.VMEM((COUNT, PART, 1, rows), F32),
            pltpu.VMEM((2 * COUNT, 1, rows), F32),
            pltpu.VMEM((RING, 1, rows), F32),
            pltpu.VMEM((2, 1, rows), F32),
            dma((2, 7, CUT)), dma((2, COUNT, CUT)),
            dma((COUNT, CUT)), dma((COUNT, CUT)),
            dma((2 * COUNT,)), dma((2 * COUNT,)),
            dma((COUNT,)), dma((COUNT,)),
            dma((2, COUNT, PART, 2)), dma((2, COUNT, PART, 2)),
            dma((COUNT,)), dma((COUNT,)),
            dma((2 * COUNT,)), dma((2 * COUNT,)),
            dma((RING,)), dma((RING,)),
            dma, dma,
        ],
        compiler_params=pltpu.CompilerParams(
            collective_id=0, has_side_effects=True, vmem_limit_bytes=44 * 1024 * 1024),
    )(images, texts, log_scale.reshape(1, 1))
    return gi, gt, loss.reshape(()), scale.reshape(())


def solution(mesh):
    spec = P(("dp", "group"), None)
    return jax.shard_map(
        body, mesh=mesh, in_specs=(spec, spec, P()),
        out_specs=(spec, spec, P(), P()), check_vma=False)
```

time: 68.1 us -> 61.6 us (0.905)
  Pallas kernels: 60.9 us -> 53.2 us
  local copies, waits for them, and re-layouts: 2.26 us -> 3.11 us
    pallas_call x1, Pallas kernels: 60.9 us -> 53.2 us  [body(): pl.pallas_call(kernel, out_shape=(jax.ShapeDtypeStruct(images.shape, imag...]
    unnamed x4 -> x6, local copies, waits for them, and re-layouts: 2.26 us -> 3.11 us
where the time goes in v2:
time: 61.6 us; the launch traced here: 61.1 us
  Pallas kernels  53.2 us (86%)
  between operations  4.79 us (8%)
  local copies, waits for them, and re-layouts  3.11 us (5%)
    pallas_call x1, Pallas kernels, body(): pl.pallas_call(kernel, out_shape=(jax.ShapeDtypeStruct(images.shape, imag...  53.2 us
    unnamed x6, local copies, waits for them, and re-layouts  3.11 us

profile of v2, /device:TPU:1, one launch (start us, length us, event | category | flops | bytes accessed | tf_op | source)
XLA Modules:
  0.0 61.1 jit_solution(451207686510492004)
XLA Ops:
  1.3 0.0 copy-start
  1.3 0.9 %copy-done = bf16[128,512]{1,0:T(8,128)(2,1)S(1)} copy-done((bf16[128,512]{1,0:T(8,128)(2,1)S(1)}, bf16[128,512]{1,0:T(8,128)(2,1)}, u32[]{:S(2)}) %copy-start) | copy-done | bytes 131096
  2.2 0.0 copy-start.1
  2.2 0.9 %copy-done.1 = bf16[128,512]{1,0:T(8,128)(2,1)S(1)} copy-done((bf16[128,512]{1,0:T(8,128)(2,1)S(1)}, bf16[128,512]{1,0:T(8,128)(2,1)}, u32[]{:S(2)}) %copy-start.1) | copy-done | bytes 131096
  3.1 53.2 %shard_map.66 = (bf16[128,512]{1,0:T(8,128)(2,1)S(1)}, bf16[128,512]{1,0:T(8,128)(2,1)S(1)}, f32[1,1]{1,0:T(1,128)}, f32[1,1]{1,0:T(1,128)}) custom-call(bf16[128,512]{1,0:T(8,128)(2,1)S(1)} %copy-done, bf16[128,512]{1,0:T(8,128)(2,1)S(1)} %copy-done.1, f32[1,1]{1,0:T(1,128)} %bitcast.3.log_scale), custom_call_target="tpu_custom_call" | custom-call | tf_op jit(solution)/shard_map/pallas_call | solution.py:460
  56.3 0.7 %copy.12 = bf16[128,512]{1,0:T(8,128)(2,1)} copy(bf16[128,512]{1,0:T(8,128)(2,1)S(1)} %get-tuple-element.16) | data formatting | bytes 262144
  57.0 0.7 %copy.13 = bf16[128,512]{1,0:T(8,128)(2,1)} copy(bf16[128,512]{1,0:T(8,128)(2,1)S(1)} %get-tuple-element.17) | data formatting | bytes 262144
Async XLA Ops:
  1.3 0.9 %copy-start = (bf16[128,512]{1,0:T(8,128)(2,1)S(1)}, bf16[128,512]{1,0:T(8,128)(2,1)}, u32[]{:S(2)}) copy-start(bf16[128,512]{1,0:T(8,128)(2,1)} %images.1) | copy-start | bytes 393220
  2.2 0.9 %copy-start.1 = (bf16[128,512]{1,0:T(8,128)(2,1)S(1)}, bf16[128,512]{1,0:T(8,128)(2,1)}, u32[]{:S(2)}) copy-start(bf16[128,512]{1,0:T(8,128)(2,1)} %texts.1) | copy-start | bytes 393220

commit v3 on v2

v3 whole, which is shorter than its diff:
```python
import functools
import math

import jax
import jax.numpy as jnp
from jax import lax
from jax.experimental import pallas as pl
from jax.experimental.pallas import tpu as pltpu
from jax.sharding import PartitionSpec as P

MESH = pl.DeviceIdType.MESH
NT = (((1,), (1,)), ((), ()))
NN = (((1,), (0,)), ((), ()))
F32 = jnp.float32
BF16 = jnp.bfloat16
LOG2E = math.log2(math.e)
LN2 = math.log(2.0)

SLOTS = ((0, 0), (1, 0), (0, 1), (0, 3), (1, 1), (1, 3), (0, 2), (1, 2))
INDEX = {slot: j for j, slot in enumerate(SLOTS)}
RING = 4
COUNT = len(SLOTS)
IMG, TXT = 0, 1
CUT = 2
PART = 2
LINE = 512
GROUPS = 40
SENDS = 4
SENT = 3 * 1024 * 1024
DEPTH = 120.0
FLIP, UP, DOWN, FLIP_UP, FLIP_DOWN, FAR, FLIP_FAR = range(7)


def back(j):
    f, o = SLOTS[j]
    return INDEX[f, (RING - o) % RING]


def seen(j, k):
    f, o = SLOTS[j]
    a, b = SLOTS[k]
    return INDEX[f ^ a, (o - b) % RING]


def kernel(
    images, texts, log_scale, gi_out, gt_out, loss_out, scale_out,
    img, img_t, txt, lone, logits, by_row, by_col, weights, row_top, row_sum, col_top, col_sum,
    row_all, col_all, row_dot, col_dot, row_gain, col_gain,
    gi, gi_far, gi_pair, gi_code, gi_top, gi_recv, gi_top_recv,
    gt, gt_code, gt_top, gt_recv, gt_top_recv, sc_one, sc_two, sc_three, ruler, load, sent, came,
):
    rows, width = images.shape
    pair = 2 * rows
    z = lax.axis_index("group")
    d = lax.axis_index("dp")
    core = lax.rem(d, 2)
    y = lax.rem(lax.div(d, 2), RING)
    x = lax.div(d, 2 * RING)
    mate = 1 - core

    def dp_of(a, b, c):
        return (a * RING + b) * 2 + c

    x_img = x + 1 - 2 * lax.rem(x, 2)
    x_txt = 3 - x

    def img_dev(f, o, k):
        return {"dp": dp_of(x_img if f else x, y, mate if k else core), "group": lax.rem(z + o, RING)}

    def txt_dev(f, o):
        return {"dp": dp_of(x_txt if f else x, lax.rem(y + o, RING), core), "group": z}

    def dev(stream, f, o):
        return img_dev(f, o, 0) if stream == IMG else txt_dev(f, o)

    groups, owed, left = {}, {}, [0] * SENDS

    def put(src, dst, group, to):
        n = groups.setdefault(group, len(groups))
        size = math.prod(src.shape) * src.dtype.itemsize
        owed[group] = owed.get(group, 0) + size
        kind = {"a": 0, "c": 0, "p": 1, "r": 2}.get(group[0], 3)
        left[kind] += size
        pltpu.make_async_remote_copy(
            src_ref=src, dst_ref=dst, send_sem=sent.at[kind], recv_sem=came.at[n], device_id=to, device_id_type=MESH).start()

    def measure(size):
        assert size % LINE == 0
        return ruler.at[pl.ds(0, size // LINE)]

    def await_all(group):
        ref = measure(owed.pop(group))
        pltpu.make_async_remote_copy(
            src_ref=ref, dst_ref=ref, send_sem=sent.at[0], recv_sem=came.at[groups[group]],
            device_id=img_dev(1, 0, 0), device_id_type=MESH).wait_recv()

    def all_img_peers():
        return [(j, k) for j in range(COUNT) for k in range(2) if (j, k) != (0, 0)]

    loads = [pltpu.make_async_copy(images, img.at[pl.ds(0, rows)], load.at[0]),
             pltpu.make_async_copy(texts, txt.at[pl.ds(0, rows)], load.at[1]),
             pltpu.make_async_copy(log_scale, lone, load.at[2])]
    for copy in loads:
        copy.start()
    barrier = pltpu.get_barrier_semaphore()
    for j, k in all_img_peers():
        pl.semaphore_signal(barrier, inc=1, device_id=img_dev(*SLOTS[j], k), device_id_type=MESH)
    for j in range(1, COUNT):
        pl.semaphore_signal(barrier, inc=1, device_id=txt_dev(*SLOTS[j]), device_id_type=MESH)
    for copy in loads:
        copy.wait()
    pl.semaphore_wait(barrier, 2 * COUNT - 1 + COUNT - 1)

    cut = rows // CUT

    def place(stream, j, h):
        return img.at[pl.ds(j * pair + h * cut, cut)] if stream == IMG else txt.at[pl.ds(j * rows + h * cut, cut)]

    def group_of(stream, j, h):
        if j in (1, 6):
            return "a", stream, j, h
        return "a", stream, {2: 2, 3: 2, 4: 4, 5: 4, 7: 7}[j]

    def a_put(stream, kind, h):
        k, j, to = {
            FLIP: (0, 1, (1, 0)),
            UP: (0, 3, (0, 1)),
            DOWN: (0, 2, (0, 3)),
            FLIP_UP: (1, 5, (0, 1)),
            FLIP_DOWN: (1, 4, (0, 3)),
            FAR: (0, 6, (0, 2)),
            FLIP_FAR: (6, 7, (1, 0)),
        }[kind]
        put(place(stream, k, h), place(stream, j, h), group_of(stream, j, h), dev(stream, *to))

    def across(j):
        put(img.at[pl.ds(j * pair, rows)], img.at[pl.ds(j * pair + rows, rows)],
            ("c", {0: 0, 1: 0, 2: 0, 3: 0, 4: 4, 5: 4, 6: 4, 7: 7}[j]), img_dev(0, 0, 1))

    for kinds in ((FLIP, FAR), (UP, DOWN)):
        for h in range(CUT):
            for kind in kinds:
                for stream in (IMG, TXT):
                    a_put(stream, kind, h)
    across(0)
    s = jnp.exp(lone[...])
    s2 = s * LOG2E

    for h in range(CUT):
        for stream in (IMG, TXT):
            await_all(("a", stream, 1, h))
            a_put(stream, FLIP_UP, h)
            a_put(stream, FLIP_DOWN, h)
        for stream in (IMG, TXT):
            await_all(("a", stream, 6, h))
            a_put(stream, FLIP_FAR, h)
    across(1)
    across(6)
    await_all(("a", IMG, 2))
    across(2)
    across(3)
    await_all(("a", TXT, 2))

    span = 4 * rows
    eye = (lax.broadcasted_iota(jnp.int32, (rows, rows), 0)
           == lax.broadcasted_iota(jnp.int32, (rows, rows), 1))

    def product(i, h):
        rr, cc = pl.ds(i * pair, pair), pl.ds(h * span, span)
        logits[rr, cc] = s2 * lax.dot_general(img[rr, :], txt[cc, :], NT, preferred_element_type=F32)

    def stats(i, h):
        rr, cc = pl.ds(i * pair, pair), pl.ds(h * span, span)
        part = logits[rr, cc]
        tiles = [part[:, t:t + rows] for t in range(0, span, rows)]
        high = functools.reduce(jnp.maximum, tiles)
        if h:
            old = row_top[rr, :]
            high = jnp.maximum(high, old)
        total = functools.reduce(jnp.add, [jnp.exp2(t - high) for t in tiles])
        if h:
            total += row_sum[rr, :] * jnp.exp2(old - high)
        row_top[rr, :] = high
        row_sum[rr, :] = total
        tall = part.reshape(pair // 8, 8, span)
        high = jnp.max(tall, axis=0)
        if i:
            old = col_top[:, cc]
            high = jnp.maximum(high, old)
        total = jnp.sum(jnp.exp2(tall - high[None]), axis=0)
        if i:
            total += col_sum[:, cc] * jnp.exp2(old - high)
        col_sum[:, cc] = total
        col_top[:, cc] = high

    def close_row(i):
        for b in (2 * i, 2 * i + 1):
            rr = pl.ds(b * rows, rows)
            top = row_top[rr, :]
            high = jnp.max(top, axis=1, keepdims=True)
            total = jnp.sum(row_sum[rr, :] * jnp.exp2(top - high), axis=1, keepdims=True)
            lse = high + jnp.log(total) * LOG2E
            row_top[rr, :] = jnp.broadcast_to(lse, top.shape)
            row_all[0, b] = jnp.sum(jnp.where(eye, lse, 0.0), axis=0, keepdims=True)

    def units(work, close):
        product(*work[0])
        for n, unit in enumerate(work):
            if n + 1 < len(work):
                product(*work[n + 1])
            stats(*unit)
            if close and unit[1]:
                close_row(unit[0])

    def turn(j):
        img_t[:, pl.ds(j * pair, pair)] = img[pl.ds(j * pair, pair), :].T

    await_all(("c", 0))
    units([(0, 0), (1, 0), (2, 0), (3, 0)], False)
    await_all(("a", IMG, 4))
    across(4)
    across(5)
    await_all(("a", TXT, 4))
    await_all(("c", 4))
    units([(4, 0), (5, 0), (6, 0)], False)
    await_all(("a", IMG, 7))
    across(7)
    await_all(("a", TXT, 7))
    await_all(("c", 7))
    units([(0, 1), (1, 1), (2, 1), (3, 1), (4, 1), (5, 1), (6, 1), (7, 0), (7, 1)], True)

    high = jnp.max(col_top[...], axis=0, keepdims=True)
    col_own = high + jnp.log(jnp.sum(col_sum[...] * jnp.exp2(col_top[...] - high), axis=0, keepdims=True)) * LOG2E
    for j in range(COUNT):
        col_all[0, j] = col_own[:, j * rows:(j + 1) * rows]
    for j in reversed(range(COUNT)):
        for k in (1, 0):
            if (j, k) != (0, 0):
                put(row_all.at[0], row_all.at[back(j) * 2 + k], ("row",), img_dev(*SLOTS[j], k))
        if j:
            put(col_all.at[0], col_all.at[back(j)], ("col",), txt_dev(*SLOTS[j]))

    def local(i):
        rr = pl.ds(i * pair, pair)
        for b in range(0, pair, rows // 2):
            rb = pl.ds(i * pair + b, rows // 2)
            line = row_top[rb, :] + 1.0
            dot = jnp.zeros(line.shape, F32)
            for t in range(0, COUNT * rows, rows):
                part = logits[rb, t:t + rows]
                e = jnp.exp2(part - line)
                by_row[rb, t:t + rows] = e
                dot += e * part
                e = jnp.exp2(part - (col_own[:, t:t + rows] + 1.0))
                by_col[rb, t:t + rows] = e
                gain = jnp.sum((e * part).reshape(rows // 16, 8, rows), axis=0)
                if i or b:
                    gain += col_dot[:, t:t + rows]
                col_dot[:, t:t + rows] = gain
            row_dot[rb, :] = dot

    for j in range(COUNT):
        local(j)
    for j in range(COUNT):
        turn(j)

    def join(values):
        high = functools.reduce(jnp.maximum, values)
        total = functools.reduce(jnp.add, [jnp.exp2(v - high) for v in values])
        return high + jnp.log(total) * LOG2E

    await_all(("col",))
    for j in range(COUNT):
        line = join([col_all[k, seen(j, k)] for k in range(COUNT)])
        if j == 0:
            own_col = line
        col_gain[0:1, j * rows:(j + 1) * rows] = jnp.exp2(col_own[:, j * rows:(j + 1) * rows] - line)
    await_all(("row",))
    for j in range(COUNT):
        for k in range(2):
            line = join([row_all[a * 2 + b, seen(j, a) * 2 + (k ^ b)] for a in range(COUNT) for b in range(2)])
            if (j, k) == (0, 0):
                own_row = line
            gain = jnp.exp2(row_all[0, j * 2 + k] - line)
            row_gain[pl.ds((j * 2 + k) * rows, rows), :] = jnp.broadcast_to(gain, (rows, rows)).T

    own = logits[0:rows, 0:rows]
    own_pairs = jnp.sum(jnp.where(eye, own, 0.0), axis=0, keepdims=True)
    loss_part = LN2 * jnp.sum(own_row + own_col - 2.0 * own_pairs, axis=1, keepdims=True)

    def weigh(i):
        for b in range(0, pair, rows // 2):
            rb = pl.ds(i * pair + b, rows // 2)
            gain = row_gain[rb, :]
            for t in range(0, COUNT * rows, rows):
                w = by_row[rb, t:t + rows] * gain + by_col[rb, t:t + rows] * col_gain[0:1, t:t + rows]
                weights[rb, t:t + rows] = w.astype(BF16)

    def weigh_own():
        w = by_row[0:rows, 0:rows] * row_gain[0:rows, :] + by_col[0:rows, 0:rows] * col_gain[0:1, 0:rows]
        weights[0:rows, 0:rows] = (w - jnp.where(eye, 1.0, 0.0)).astype(BF16)

    me_one = (lax.rem(x, 2) * RING + z) * 2 + core
    half = lax.div(x, 2)
    first = lax.broadcasted_iota(jnp.int32, (1, rows), 1) == 0

    def scalar_one():
        rest = jnp.sum((row_dot[...] * row_gain[...]).reshape(2 * COUNT * rows // 8, 8, rows), axis=0)
        gain = col_dot[...] * col_gain[...]
        for t in range(0, COUNT * rows, rows):
            rest += gain[:, t:t + rows]
        rest = jnp.sum(rest, axis=0, keepdims=True)
        scale_part = LN2 * jnp.sum(rest - own_pairs, axis=1, keepdims=True)
        sc_one[me_one] = jnp.where(first, loss_part, scale_part)
        for j, k in all_img_peers():
            put(sc_one.at[me_one], sc_one.at[me_one], ("one",), img_dev(*SLOTS[j], k))

    def scalar_two():
        await_all(("one",))
        sc_two[y] = jnp.sum(sc_one[...], axis=0)
        for o in range(1, RING):
            put(sc_two.at[y], sc_two.at[y], ("two",), txt_dev(0, o))

    def scalar_three():
        await_all(("two",))
        sc_three[half] = jnp.sum(sc_two[...], axis=0)
        put(sc_three.at[half], sc_three.at[half], ("three",), txt_dev(1, 0))

    def gi_blocks(j):
        part = lax.dot_general(weights[pl.ds(j * pair, 2 * pair), :], txt[...], NN, preferred_element_type=F32)
        for k in range(2):
            gi[j + k] = part[k * pair:k * pair + rows]
            gi_far[j + k] = part[k * pair + rows:(k + 1) * pair]
            put(gi_far.at[j + k], gi_pair.at[j + k], ("p", j), img_dev(0, 0, 1))

    def pair_sum(j):
        if ("p", j) in owed:
            await_all(("p", j))
        gi[j] += gi_pair[j]

    def gt_half(h):
        part = lax.dot_general(img_t[...], weights[:, pl.ds(h * span, span)], NN, preferred_element_type=F32)
        for j in range(4):
            gt[4 * h + j] = part[:, j * rows:(j + 1) * rows]

    sums = (gi, gt)
    codes = (gi_code, gt_code)
    tops = (gi_top, gt_top)
    code_in = (gi_recv, gt_recv)
    top_in = (gi_top_recv, gt_top_recv)
    target = {7: (1, 0), 4: (0, 1), 5: (0, 3), 2: (0, 1), 3: (0, 3), 6: (0, 2), 1: (1, 0)}

    def part_of(stream, h):
        n = sums[stream].shape[1] // PART
        return pl.ds(h * n, n)

    def r_group(stream, j, h):
        return ("r", stream, 4 if j == 5 else j, h) if j in (7, 4, 5) else ("r", stream, 2 if j == 3 else j)

    def arrived(stream, j, h):
        group = r_group(stream, j, h)
        if group in owed:
            await_all(group)

    def give(stream, j, h, total):
        top = jnp.maximum(jnp.max(jnp.abs(total), axis=0, keepdims=True), 1e-30)
        codes[stream][j, part_of(stream, h)] = jnp.exp2(total * (DEPTH / top)).astype(BF16)
        tops[stream][j, h] = top * (LOG2E / DEPTH)
        hh = part_of(stream, h)
        to = dev(stream, *target[j])
        put(codes[stream].at[j, hh], code_in[stream].at[j, hh], r_group(stream, j, h), to)
        put(tops[stream].at[j, h], top_in[stream].at[j, h], r_group(stream, j, h), to)

    def take(stream, j, h):
        arrived(stream, j, h)
        return jnp.log(code_in[stream][j, part_of(stream, h)].astype(F32)) * top_in[stream][j, h]

    def send(stream, *slots):
        for j in slots:
            for h in range(PART):
                give(stream, j, h, sums[stream][j, part_of(stream, h)])

    def send_on(stream, j, sources):
        for h in range(PART):
            total = sums[stream][j, part_of(stream, h)]
            for k in sources:
                total += take(stream, k, h)
            give(stream, j, h, total)

    for j in range(COUNT):
        weigh(j)
    weigh_own()
    gi_blocks(4)
    gi_blocks(6)
    gt_half(1)
    for j in (4, 5):
        pair_sum(j)
        send(IMG, j)
    send(TXT, 4, 5, 7)
    pair_sum(6)
    pair_sum(7)
    send(IMG, 7)
    scalar_one()
    gt_half(0)
    send(TXT, 2, 3)
    gi_blocks(2)
    gi_blocks(0)
    scalar_two()
    for j in (2, 3):
        pair_sum(j)
        send(IMG, j)
    pair_sum(0)
    pair_sum(1)
    send_on(TXT, 6, (7,))
    send_on(IMG, 6, (7,))
    send_on(IMG, 1, (4, 5))
    send_on(TXT, 1, (4, 5))
    scalar_three()

    def finish(stream):
        out = []
        for h in range(PART):
            total = sums[stream][0, part_of(stream, h)]
            for j in (2, 3, 6, 1):
                total += take(stream, j, h)
            out.append(s * total)
        return jnp.concatenate(out, axis=0)

    gt_out[...] = finish(TXT).T.astype(gt_out.dtype)
    gi_out[...] = finish(IMG).astype(gi_out.dtype)
    await_all(("three",))
    total = sc_three[0] + sc_three[1]
    pair_total = 2 * RING * RING * RING * rows
    loss_out[...] = total[0:1, 0:1] / (2.0 * pair_total)
    scale_out[...] = total[0:1, 1:2] / pair_total

    for kind in range(SENDS):
        ref = measure(left[kind])
        pltpu.make_async_remote_copy(
            src_ref=ref, dst_ref=ref, send_sem=sent.at[kind], recv_sem=came.at[0],
            device_id=img_dev(1, 0, 0), device_id_type=MESH).wait_send()
    assert not owed and len(groups) == GROUPS, (owed, len(groups), left)


def body(images, texts, log_scale):
    rows, width = images.shape
    vmem = pl.BlockSpec(memory_space=pltpu.VMEM)
    dma = pltpu.SemaphoreType.DMA
    gi, gt, loss, scale = pl.pallas_call(
        kernel,
        out_shape=(
            jax.ShapeDtypeStruct(images.shape, images.dtype),
            jax.ShapeDtypeStruct(texts.shape, texts.dtype),
            jax.ShapeDtypeStruct((1, 1), F32),
            jax.ShapeDtypeStruct((1, 1), F32),
        ),
        in_specs=[pl.BlockSpec(memory_space=pltpu.HBM)] * 3,
        out_specs=(vmem,) * 4,
        scratch_shapes=[
            pltpu.VMEM((2 * COUNT * rows, width), BF16),
            pltpu.VMEM((width, 2 * COUNT * rows), BF16),
            pltpu.VMEM((COUNT * rows, width), BF16),
            pltpu.VMEM((1, 1), F32),
            pltpu.VMEM((2 * COUNT * rows, COUNT * rows), F32),
            pltpu.VMEM((2 * COUNT * rows, COUNT * rows), F32),
            pltpu.VMEM((2 * COUNT * rows, COUNT * rows), F32),
            pltpu.VMEM((2 * COUNT * rows, COUNT * rows), BF16),
            pltpu.VMEM((2 * COUNT * rows, rows), F32),
            pltpu.VMEM((2 * COUNT * rows, rows), F32),
            pltpu.VMEM((8, COUNT * rows), F32),
            pltpu.VMEM((8, COUNT * rows), F32),
            pltpu.VMEM((2 * COUNT, 2 * COUNT, 1, rows), F32),
            pltpu.VMEM((COUNT, COUNT, 1, rows), F32),
            pltpu.VMEM((2 * COUNT * rows, rows), F32),
            pltpu.VMEM((8, COUNT * rows), F32),
            pltpu.VMEM((2 * COUNT * rows, rows), F32),
            pltpu.VMEM((1, COUNT * rows), F32),
            pltpu.VMEM((COUNT, rows, width), F32),
            pltpu.VMEM((COUNT, rows, width), F32),
            pltpu.VMEM((COUNT, rows, width), F32),
            pltpu.VMEM((COUNT, rows, width), BF16),
            pltpu.VMEM((COUNT, PART, 1, width), F32),
            pltpu.VMEM((COUNT, rows, width), BF16),
            pltpu.VMEM((COUNT, PART, 1, width), F32),
            pltpu.VMEM((COUNT, width, rows), F32),
            pltpu.VMEM((COUNT, width, rows), BF16),
            pltpu.VMEM((COUNT, PART, 1, rows), F32),
            pltpu.VMEM((COUNT, width, rows), BF16),
            pltpu.VMEM((COUNT, PART, 1, rows), F32),
            pltpu.VMEM((2 * COUNT, 1, rows), F32),
            pltpu.VMEM((RING, 1, rows), F32),
            pltpu.VMEM((2, 1, rows), F32),
            pltpu.VMEM((SENT // LINE, 1, rows), F32),
            dma((3,)), dma((SENDS,)), dma((GROUPS,)),
        ],
        compiler_params=pltpu.CompilerParams(
            collective_id=0, has_side_effects=True, vmem_limit_bytes=53 * 1024 * 1024),
    )(images, texts, log_scale.reshape(1, 1))
    return gi, gt, loss.reshape(()), scale.reshape(())


def solution(mesh):
    spec = P(("dp", "group"), None)
    return jax.shard_map(
        body, mesh=mesh, in_specs=(spec, spec, P()),
        out_specs=(spec, spec, P(), P()), check_vma=False)
```

time: 61.6 us -> 59.4 us (0.964)
  Pallas kernels: 53.2 us -> 51.3 us
    pallas_call x1, Pallas kernels: 53.2 us -> 51.3 us  [body(): pl.pallas_call(kernel, out_shape=(jax.ShapeDtypeStruct(images.shape, imag...]
where the time goes in v3:
time: 59.4 us; the launch traced here: 59.3 us
  Pallas kernels  51.3 us (86%)
  between operations  4.79 us (8%)
  local copies, waits for them, and re-layouts  3.11 us (5%)
    pallas_call x1, Pallas kernels, body(): pl.pallas_call(kernel, out_shape=(jax.ShapeDtypeStruct(images.shape, imag...  51.3 us
    unnamed x6, local copies, waits for them, and re-layouts  3.11 us

profile of v3, /device:TPU:1, one launch (start us, length us, event | category | flops | bytes accessed | tf_op | source)
XLA Modules:
  0.0 59.3 jit_solution(6935961634694801350)
XLA Ops:
  1.3 0.0 copy-start
  1.3 0.9 %copy-done = bf16[128,512]{1,0:T(8,128)(2,1)S(1)} copy-done((bf16[128,512]{1,0:T(8,128)(2,1)S(1)}, bf16[128,512]{1,0:T(8,128)(2,1)}, u32[]{:S(2)}) %copy-start) | copy-done | bytes 131096
  2.2 0.0 copy-start.1
  2.2 0.9 %copy-done.1 = bf16[128,512]{1,0:T(8,128)(2,1)S(1)} copy-done((bf16[128,512]{1,0:T(8,128)(2,1)S(1)}, bf16[128,512]{1,0:T(8,128)(2,1)}, u32[]{:S(2)}) %copy-start.1) | copy-done | bytes 131096
  3.1 51.3 %shard_map.66 = (bf16[128,512]{1,0:T(8,128)(2,1)S(1)}, bf16[128,512]{1,0:T(8,128)(2,1)S(1)}, f32[1,1]{1,0:T(1,128)}, f32[1,1]{1,0:T(1,128)}) custom-call(bf16[128,512]{1,0:T(8,128)(2,1)S(1)} %copy-done, bf16[128,512]{1,0:T(8,128)(2,1)S(1)} %copy-done.1, f32[1,1]{1,0:T(1,128)} %bitcast.3.log_scale), custom_call_target="tpu_custom_call" | custom-call | tf_op jit(solution)/shard_map/pallas_call | solution.py:449
  54.4 0.7 %copy.12 = bf16[128,512]{1,0:T(8,128)(2,1)} copy(bf16[128,512]{1,0:T(8,128)(2,1)S(1)} %get-tuple-element.16) | data formatting | bytes 262144
  55.1 0.7 %copy.13 = bf16[128,512]{1,0:T(8,128)(2,1)} copy(bf16[128,512]{1,0:T(8,128)(2,1)S(1)} %get-tuple-element.17) | data formatting | bytes 262144
Async XLA Ops:
  1.3 0.9 %copy-start = (bf16[128,512]{1,0:T(8,128)(2,1)S(1)}, bf16[128,512]{1,0:T(8,128)(2,1)}, u32[]{:S(2)}) copy-start(bf16[128,512]{1,0:T(8,128)(2,1)} %images.1) | copy-start | bytes 393220
  2.2 0.9 %copy-start.1 = (bf16[128,512]{1,0:T(8,128)(2,1)S(1)}, bf16[128,512]{1,0:T(8,128)(2,1)}, u32[]{:S(2)}) copy-start(bf16[128,512]{1,0:T(8,128)(2,1)} %texts.1) | copy-start | bytes 393220

commit v4 on v3

--- a/solution.py
+++ b/solution.py
@@ -24,7 +24,7 @@
 CUT = 2
 PART = 2
 LINE = 512
-GROUPS = 40
+GROUPS = 41
 SENDS = 4
 SENT = 3 * 1024 * 1024
 DEPTH = 120.0
@@ -135,7 +135,7 @@
 
     def across(j):
         put(img.at[pl.ds(j * pair, rows)], img.at[pl.ds(j * pair + rows, rows)],
-            ("c", {0: 0, 1: 0, 2: 0, 3: 0, 4: 4, 5: 4, 6: 4, 7: 7}[j]), img_dev(0, 0, 1))
+            ("c", {0: 0, 1: 0, 2: 2, 3: 2, 4: 4, 5: 4, 6: 4, 7: 7}[j]), img_dev(0, 0, 1))
 
     for kinds in ((FLIP, FAR), (UP, DOWN)):
         for h in range(CUT):
@@ -165,24 +165,24 @@
     eye = (lax.broadcasted_iota(jnp.int32, (rows, rows), 0)
            == lax.broadcasted_iota(jnp.int32, (rows, rows), 1))
 
-    def product(i, h):
-        rr, cc = pl.ds(i * pair, pair), pl.ds(h * span, span)
+    def product(i, c0, cols):
+        rr, cc = pl.ds(i * pair, pair), pl.ds(c0, cols)
         logits[rr, cc] = s2 * lax.dot_general(img[rr, :], txt[cc, :], NT, preferred_element_type=F32)
 
-    def stats(i, h):
-        rr, cc = pl.ds(i * pair, pair), pl.ds(h * span, span)
+    def stats(i, c0, cols):
+        rr, cc = pl.ds(i * pair, pair), pl.ds(c0, cols)
         part = logits[rr, cc]
-        tiles = [part[:, t:t + rows] for t in range(0, span, rows)]
+        tiles = [part[:, t:t + rows] for t in range(0, cols, rows)]
         high = functools.reduce(jnp.maximum, tiles)
-        if h:
+        if c0:
             old = row_top[rr, :]
             high = jnp.maximum(high, old)
         total = functools.reduce(jnp.add, [jnp.exp2(t - high) for t in tiles])
-        if h:
+        if c0:
             total += row_sum[rr, :] * jnp.exp2(old - high)
         row_top[rr, :] = high
         row_sum[rr, :] = total
-        tall = part.reshape(pair // 8, 8, span)
+        tall = part.reshape(pair // 8, 8, cols)
         high = jnp.max(tall, axis=0)
         if i:
             old = col_top[:, cc]
@@ -203,31 +203,36 @@
             row_top[rr, :] = jnp.broadcast_to(lse, top.shape)
             row_all[0, b] = jnp.sum(jnp.where(eye, lse, 0.0), axis=0, keepdims=True)
 
-    def units(work, close):
+    def units(work):
         product(*work[0])
         for n, unit in enumerate(work):
             if n + 1 < len(work):
                 product(*work[n + 1])
             stats(*unit)
-            if close and unit[1]:
+            if unit[1] + unit[2] == COUNT * rows:
                 close_row(unit[0])
 
     def turn(j):
         img_t[:, pl.ds(j * pair, pair)] = img[pl.ds(j * pair, pair), :].T
 
     await_all(("c", 0))
-    units([(0, 0), (1, 0), (2, 0), (3, 0)], False)
+    units([(0, 0, span), (1, 0, span)])
+    await_all(("c", 2))
+    units([(2, 0, span), (3, 0, span)])
     await_all(("a", IMG, 4))
     across(4)
     across(5)
     await_all(("a", TXT, 4))
+    units([(i, span, pair) for i in (0, 1, 2, 3)])
     await_all(("c", 4))
-    units([(4, 0), (5, 0), (6, 0)], False)
     await_all(("a", IMG, 7))
     across(7)
+    units([(i, 0, span) for i in (4, 5, 6)] + [(i, span, pair) for i in (4, 5, 6)])
+    for j in range(COUNT - 1):
+        turn(j)
     await_all(("a", TXT, 7))
     await_all(("c", 7))
-    units([(0, 1), (1, 1), (2, 1), (3, 1), (4, 1), (5, 1), (6, 1), (7, 0), (7, 1)], True)
+    units([(i, span + pair, pair) for i in range(7)] + [(7, 0, span), (7, span, span)])
 
     high = jnp.max(col_top[...], axis=0, keepdims=True)
     col_own = high + jnp.log(jnp.sum(col_sum[...] * jnp.exp2(col_top[...] - high), axis=0, keepdims=True)) * LOG2E
@@ -261,8 +266,7 @@
 
     for j in range(COUNT):
         local(j)
-    for j in range(COUNT):
-        turn(j)
+    turn(COUNT - 1)
 
     def join(values):
         high = functools.reduce(jnp.maximum, values)
@@ -312,6 +316,8 @@
         rest = jnp.sum(rest, axis=0, keepdims=True)
         scale_part = LN2 * jnp.sum(rest - own_pairs, axis=1, keepdims=True)
         sc_one[me_one] = jnp.where(first, loss_part, scale_part)
+
+    def scalar_send():
         for j, k in all_img_peers():
             put(sc_one.at[me_one], sc_one.at[me_one], ("one",), img_dev(*SLOTS[j], k))
 
@@ -331,11 +337,14 @@
         for k in range(2):
             gi[j + k] = part[k * pair:k * pair + rows]
             gi_far[j + k] = part[k * pair + rows:(k + 1) * pair]
+
+    def gi_across(j):
+        for k in range(2):
             put(gi_far.at[j + k], gi_pair.at[j + k], ("p", j), img_dev(0, 0, 1))
 
     def pair_sum(j):
-        if ("p", j) in owed:
-            await_all(("p", j))
+        if ("p", j - j % 2) in owed:
+            await_all(("p", j - j % 2))
         gi[j] += gi_pair[j]
 
     def gt_half(h):
@@ -380,41 +389,49 @@
             for h in range(PART):
                 give(stream, j, h, sums[stream][j, part_of(stream, h)])
 
-    def send_on(stream, j, sources):
-        for h in range(PART):
-            total = sums[stream][j, part_of(stream, h)]
-            for k in sources:
-                total += take(stream, k, h)
-            give(stream, j, h, total)
-
-    for j in range(COUNT):
+    def send_on(stream, j, sources, h):
+        total = sums[stream][j, part_of(stream, h)]
+        for k in sources:
+            total += take(stream, k, h)
+        give(stream, j, h, total)
+
+    weigh(4)
+    weigh(5)
+    gi_blocks(4)
+    for j in (6, 7, 0, 1, 2, 3):
         weigh(j)
     weigh_own()
-    gi_blocks(4)
-    gi_blocks(6)
+    scalar_one()
+    gi_across(4)
+    scalar_send()
     gt_half(1)
+    send(TXT, 4, 5, 7)
     for j in (4, 5):
         pair_sum(j)
         send(IMG, j)
-    send(TXT, 4, 5, 7)
+    gi_blocks(6)
+    gi_across(6)
+    gi_blocks(2)
+    gi_across(2)
     pair_sum(6)
     pair_sum(7)
     send(IMG, 7)
-    scalar_one()
     gt_half(0)
     send(TXT, 2, 3)
-    gi_blocks(2)
-    gi_blocks(0)
-    scalar_two()
     for j in (2, 3):
         pair_sum(j)
         send(IMG, j)
+    gi_blocks(0)
+    gi_across(0)
+    scalar_two()
+    for h in range(PART):
+        send_on(TXT, 6, (7,), h)
+        send_on(TXT, 1, (4, 5), h)
+    pair_sum(1)
     pair_sum(0)
-    pair_sum(1)
-    send_on(TXT, 6, (7,))
-    send_on(IMG, 6, (7,))
-    send_on(IMG, 1, (4, 5))
-    send_on(TXT, 1, (4, 5))
+    for h in range(PART):
+        send_on(IMG, 6, (7,), h)
+        send_on(IMG, 1, (4, 5), h)
     scalar_three()
 
     def finish(stream):
@@ -494,7 +511,7 @@
             dma((3,)), dma((SENDS,)), dma((GROUPS,)),
         ],
         compiler_params=pltpu.CompilerParams(
-            collective_id=0, has_side_effects=True, vmem_limit_bytes=53 * 1024 * 1024),
+            collective_id=0, has_side_effects=True, vmem_limit_bytes=54880 * 1024),
     )(images, texts, log_scale.reshape(1, 1))
     return gi, gt, loss.reshape(()), scale.reshape(())
 

time: 59.4 us -> 53.8 us (0.906)
  Pallas kernels: 51.3 us -> 47.1 us
  local copies, waits for them, and re-layouts: 3.11 us -> 1.31 us
    pallas_call x1, Pallas kernels: 51.3 us -> 47.1 us  [body(): pl.pallas_call(kernel, out_shape=(jax.ShapeDtypeStruct(images.shape, imag...]
    unnamed x6 -> x2, local copies, waits for them, and re-layouts: 3.11 us -> 1.31 us
where the time goes in v4:
time: 53.8 us; the launch traced here: 53.1 us
  Pallas kernels  47.1 us (88%)
  between operations  4.74 us (9%)
  local copies, waits for them, and re-layouts  1.31 us (2%)
    pallas_call x1, Pallas kernels, body(): pl.pallas_call(kernel, out_shape=(jax.ShapeDtypeStruct(images.shape, imag...  47.1 us
    unnamed x2, local copies, waits for them, and re-layouts  1.31 us

profile of v4, /device:TPU:1, one launch (start us, length us, event | category | flops | bytes accessed | tf_op | source)
XLA Modules:
  0.0 53.1 jit_solution(2723201845406815492)
XLA Ops:
  1.3 47.1 %shard_map.66 = (bf16[128,512]{1,0:T(8,128)(2,1)S(1)}, bf16[128,512]{1,0:T(8,128)(2,1)S(1)}, f32[1,1]{1,0:T(1,128)}, f32[1,1]{1,0:T(1,128)}) custom-call(bf16[128,512]{1,0:T(8,128)(2,1)} %images.1, bf16[128,512]{1,0:T(8,128)(2,1)} %texts.1, f32[1,1]{1,0:T(1,128)} %bitcast.3.log_scale), custom_call_target="tpu_custom_call" | custom-call | tf_op jit(solution)/shard_map/pallas_call | solution.py:466
  48.4 0.7 %copy.12 = bf16[128,512]{1,0:T(8,128)(2,1)} copy(bf16[128,512]{1,0:T(8,128)(2,1)S(1)} %get-tuple-element.16) | data formatting | bytes 262144
  49.0 0.7 %copy.13 = bf16[128,512]{1,0:T(8,128)(2,1)} copy(bf16[128,512]{1,0:T(8,128)(2,1)S(1)} %get-tuple-element.17) | data formatting | bytes 262144

commit v5 on v4

--- a/solution.py
+++ b/solution.py
@@ -97,6 +97,7 @@
     def all_img_peers():
         return [(j, k) for j in range(COUNT) for k in range(2) if (j, k) != (0, 0)]
 
+    pl.delay(1)
     loads = [pltpu.make_async_copy(images, img.at[pl.ds(0, rows)], load.at[0]),
              pltpu.make_async_copy(texts, txt.at[pl.ds(0, rows)], load.at[1]),
              pltpu.make_async_copy(log_scale, lone, load.at[2])]
@@ -137,6 +138,7 @@
         put(img.at[pl.ds(j * pair, rows)], img.at[pl.ds(j * pair + rows, rows)],
             ("c", {0: 0, 1: 0, 2: 2, 3: 2, 4: 4, 5: 4, 6: 4, 7: 7}[j]), img_dev(0, 0, 1))
 
+    pl.delay(1)
     for kinds in ((FLIP, FAR), (UP, DOWN)):
         for h in range(CUT):
             for kind in kinds:
@@ -146,6 +148,7 @@
     s = jnp.exp(lone[...])
     s2 = s * LOG2E
 
+    pl.delay(1)
     for h in range(CUT):
         for stream in (IMG, TXT):
             await_all(("a", stream, 1, h))
@@ -156,6 +159,7 @@
             a_put(stream, FLIP_FAR, h)
     across(1)
     across(6)
+    pl.delay(1)
     await_all(("a", IMG, 2))
     across(2)
     across(3)
@@ -215,25 +219,35 @@
     def turn(j):
         img_t[:, pl.ds(j * pair, pair)] = img[pl.ds(j * pair, pair), :].T
 
+    pl.delay(1)
     await_all(("c", 0))
+    pl.delay(1)
     units([(0, 0, span), (1, 0, span)])
+    pl.delay(1)
     await_all(("c", 2))
+    pl.delay(1)
     units([(2, 0, span), (3, 0, span)])
+    pl.delay(1)
     await_all(("a", IMG, 4))
     across(4)
     across(5)
     await_all(("a", TXT, 4))
+    pl.delay(1)
     units([(i, span, pair) for i in (0, 1, 2, 3)])
+    pl.delay(1)
     await_all(("c", 4))
+    pl.delay(1)
     await_all(("a", IMG, 7))
     across(7)
+    pl.delay(1)
     units([(i, 0, span) for i in (4, 5, 6)] + [(i, span, pair) for i in (4, 5, 6)])
-    for j in range(COUNT - 1):
-        turn(j)
+    pl.delay(1)
     await_all(("a", TXT, 7))
     await_all(("c", 7))
+    pl.delay(1)
     units([(i, span + pair, pair) for i in range(7)] + [(7, 0, span), (7, span, span)])
 
+    pl.delay(1)
     high = jnp.max(col_top[...], axis=0, keepdims=True)
     col_own = high + jnp.log(jnp.sum(col_sum[...] * jnp.exp2(col_top[...] - high), axis=0, keepdims=True)) * LOG2E
     for j in range(COUNT):
@@ -245,6 +259,7 @@
         if j:
             put(col_all.at[0], col_all.at[back(j)], ("col",), txt_dev(*SLOTS[j]))
 
+    pl.delay(1)
     def local(i):
         rr = pl.ds(i * pair, pair)
         for b in range(0, pair, rows // 2):
@@ -266,20 +281,25 @@
 
     for j in range(COUNT):
         local(j)
-    turn(COUNT - 1)
+    pl.delay(1)
+    for j in range(COUNT):
+        turn(j)
 
     def join(values):
         high = functools.reduce(jnp.maximum, values)
         total = functools.reduce(jnp.add, [jnp.exp2(v - high) for v in values])
         return high + jnp.log(total) * LOG2E
 
+    pl.delay(1)
     await_all(("col",))
     for j in range(COUNT):
         line = join([col_all[k, seen(j, k)] for k in range(COUNT)])
         if j == 0:
             own_col = line
         col_gain[0:1, j * rows:(j + 1) * rows] = jnp.exp2(col_own[:, j * rows:(j + 1) * rows] - line)
+    pl.delay(1)
     await_all(("row",))
+    pl.delay(1)
     for j in range(COUNT):
         for k in range(2):
             line = join([row_all[a * 2 + b, seen(j, a) * 2 + (k ^ b)] for a in range(COUNT) for b in range(2)])
@@ -288,6 +308,7 @@
             gain = jnp.exp2(row_all[0, j * 2 + k] - line)
             row_gain[pl.ds((j * 2 + k) * rows, rows), :] = jnp.broadcast_to(gain, (rows, rows)).T
 
+    pl.delay(1)
     own = logits[0:rows, 0:rows]
     own_pairs = jnp.sum(jnp.where(eye, own, 0.0), axis=0, keepdims=True)
     loss_part = LN2 * jnp.sum(own_row + own_col - 2.0 * own_pairs, axis=1, keepdims=True)
@@ -395,43 +416,59 @@
             total += take(stream, k, h)
         give(stream, j, h, total)
 
-    weigh(4)
-    weigh(5)
+    pl.delay(1)
+    weigh(6)
+    weigh(7)
+    pl.delay(1)
+    gi_blocks(6)
+    for j in (4, 5, 2, 3):
+        weigh(j)
+    gi_across(6)
+    pl.delay(1)
     gi_blocks(4)
-    for j in (6, 7, 0, 1, 2, 3):
+    for j in (0, 1):
         weigh(j)
     weigh_own()
+    gi_across(4)
+    pl.delay(1)
+    gt_half(1)
     scalar_one()
-    gi_across(4)
     scalar_send()
-    gt_half(1)
-    send(TXT, 4, 5, 7)
+    pl.delay(1)
+    send(TXT, 7, 4, 5)
+    pl.delay(1)
+    pair_sum(6)
+    pair_sum(7)
+    send(IMG, 7)
+    pl.delay(1)
     for j in (4, 5):
         pair_sum(j)
         send(IMG, j)
-    gi_blocks(6)
-    gi_across(6)
+    pl.delay(1)
     gi_blocks(2)
     gi_across(2)
-    pair_sum(6)
-    pair_sum(7)
-    send(IMG, 7)
+    pl.delay(1)
     gt_half(0)
     send(TXT, 2, 3)
+    pl.delay(1)
     for j in (2, 3):
         pair_sum(j)
         send(IMG, j)
+    pl.delay(1)
     gi_blocks(0)
     gi_across(0)
+    pl.delay(1)
     scalar_two()
+    pl.delay(1)
     for h in range(PART):
         send_on(TXT, 6, (7,), h)
         send_on(TXT, 1, (4, 5), h)
-    pair_sum(1)
-    pair_sum(0)
-    for h in range(PART):
         send_on(IMG, 6, (7,), h)
+        if h == 0:
+            pair_sum(0)
+            pair_sum(1)
         send_on(IMG, 1, (4, 5), h)
+    pl.delay(1)
     scalar_three()
 
     def finish(stream):
@@ -443,20 +480,25 @@
             out.append(s * total)
         return jnp.concatenate(out, axis=0)
 
+    pl.delay(1)
     gt_out[...] = finish(TXT).T.astype(gt_out.dtype)
+    pl.delay(1)
     gi_out[...] = finish(IMG).astype(gi_out.dtype)
+    pl.delay(1)
     await_all(("three",))
     total = sc_three[0] + sc_three[1]
     pair_total = 2 * RING * RING * RING * rows
     loss_out[...] = total[0:1, 0:1] / (2.0 * pair_total)
     scale_out[...] = total[0:1, 1:2] / pair_total
 
+    pl.delay(1)
     for kind in range(SENDS):
         ref = measure(left[kind])
         pltpu.make_async_remote_copy(
             src_ref=ref, dst_ref=ref, send_sem=sent.at[kind], recv_sem=came.at[0],
             device_id=img_dev(1, 0, 0), device_id_type=MESH).wait_send()
     assert not owed and len(groups) == GROUPS, (owed, len(groups), left)
+    pl.delay(1)
 
 
 def body(images, texts, log_scale):

time: 53.8 us -> 51.3 us (0.954)
  Pallas kernels: 47.1 us -> 45.1 us
    pallas_call x1, Pallas kernels: 47.1 us -> 45.1 us  [body(): pl.pallas_call(kernel, out_shape=(jax.ShapeDtypeStruct(images.shape, imag...]
where the time goes in v5:
time: 51.3 us; the launch traced here: 51.1 us
  Pallas kernels  45.1 us (88%)
  between operations  4.74 us (9%)
  local copies, waits for them, and re-layouts  1.31 us (3%)
    pallas_call x1, Pallas kernels, body(): pl.pallas_call(kernel, out_shape=(jax.ShapeDtypeStruct(images.shape, imag...  45.1 us
    unnamed x2, local copies, waits for them, and re-layouts  1.31 us

profile of v5, /device:TPU:1, one launch (start us, length us, event | category | flops | bytes accessed | tf_op | source)
XLA Modules:
  0.0 51.1 jit_solution(9329328187111275111)
XLA Ops:
  1.3 45.1 %shard_map.66 = (bf16[128,512]{1,0:T(8,128)(2,1)S(1)}, bf16[128,512]{1,0:T(8,128)(2,1)S(1)}, f32[1,1]{1,0:T(1,128)}, f32[1,1]{1,0:T(1,128)}) custom-call(bf16[128,512]{1,0:T(8,128)(2,1)} %images.1, bf16[128,512]{1,0:T(8,128)(2,1)} %texts.1, f32[1,1]{1,0:T(1,128)} %bitcast.3.log_scale), custom_call_target="tpu_custom_call" | custom-call | tf_op jit(solution)/shard_map/pallas_call | solution.py:508
  46.3 0.7 %copy.12 = bf16[128,512]{1,0:T(8,128)(2,1)} copy(bf16[128,512]{1,0:T(8,128)(2,1)S(1)} %get-tuple-element.16) | data formatting | bytes 262144
  47.0 0.7 %copy.13 = bf16[128,512]{1,0:T(8,128)(2,1)} copy(bf16[128,512]{1,0:T(8,128)(2,1)S(1)} %get-tuple-element.17) | data formatting | bytes 262144

commit v6 on v5

--- a/solution.py
+++ b/solution.py
@@ -104,13 +104,13 @@
     for copy in loads:
         copy.start()
     barrier = pltpu.get_barrier_semaphore()
-    for j, k in all_img_peers():
+    for j, k in ((0, 1), (1, 0), (2, 0), (3, 0), (6, 0)):
         pl.semaphore_signal(barrier, inc=1, device_id=img_dev(*SLOTS[j], k), device_id_type=MESH)
-    for j in range(1, COUNT):
+    for j in (1, 2, 3, 6):
         pl.semaphore_signal(barrier, inc=1, device_id=txt_dev(*SLOTS[j]), device_id_type=MESH)
     for copy in loads:
         copy.wait()
-    pl.semaphore_wait(barrier, 2 * COUNT - 1 + COUNT - 1)
+    pl.semaphore_wait(barrier, 9)
 
     cut = rows // CUT
 

time: 51.3 us -> 50.4 us (0.982)
  Pallas kernels: 45.1 us -> 44.2 us
    pallas_call x1, Pallas kernels: 45.1 us -> 44.2 us  [body(): pl.pallas_call(kernel, out_shape=(jax.ShapeDtypeStruct(images.shape, imag...]
where the time goes in v6:
time: 50.4 us; the launch traced here: 50.2 us
  Pallas kernels  44.2 us (88%)
  between operations  4.74 us (9%)
  local copies, waits for them, and re-layouts  1.31 us (3%)
    pallas_call x1, Pallas kernels, body(): pl.pallas_call(kernel, out_shape=(jax.ShapeDtypeStruct(images.shape, imag...  44.2 us
    unnamed x2, local copies, waits for them, and re-layouts  1.31 us

profile of v6, /device:TPU:1, one launch (start us, length us, event | category | flops | bytes accessed | tf_op | source)
XLA Modules:
  0.0 50.2 jit_solution(8724058668504504274)
XLA Ops:
  1.3 44.2 %shard_map.66 = (bf16[128,512]{1,0:T(8,128)(2,1)S(1)}, bf16[128,512]{1,0:T(8,128)(2,1)S(1)}, f32[1,1]{1,0:T(1,128)}, f32[1,1]{1,0:T(1,128)}) custom-call(bf16[128,512]{1,0:T(8,128)(2,1)} %images.1, bf16[128,512]{1,0:T(8,128)(2,1)} %texts.1, f32[1,1]{1,0:T(1,128)} %bitcast.3.log_scale), custom_call_target="tpu_custom_call" | custom-call | tf_op jit(solution)/shard_map/pallas_call | solution.py:508
  45.4 0.7 %copy.12 = bf16[128,512]{1,0:T(8,128)(2,1)} copy(bf16[128,512]{1,0:T(8,128)(2,1)S(1)} %get-tuple-element.16) | data formatting | bytes 262144
  46.1 0.7 %copy.13 = bf16[128,512]{1,0:T(8,128)(2,1)} copy(bf16[128,512]{1,0:T(8,128)(2,1)S(1)} %get-tuple-element.17) | data formatting | bytes 262144

commit v7 on v6

--- a/solution.py
+++ b/solution.py
@@ -43,7 +43,7 @@
 
 
 def kernel(
-    images, texts, log_scale, gi_out, gt_out, loss_out, scale_out,
+    images, texts, log_scale, g_out, loss_out, scale_out,
     img, img_t, txt, lone, logits, by_row, by_col, weights, row_top, row_sum, col_top, col_sum,
     row_all, col_all, row_dot, col_dot, row_gain, col_gain,
     gi, gi_far, gi_pair, gi_code, gi_top, gi_recv, gi_top_recv,
@@ -136,7 +136,7 @@
 
     def across(j):
         put(img.at[pl.ds(j * pair, rows)], img.at[pl.ds(j * pair + rows, rows)],
-            ("c", {0: 0, 1: 0, 2: 2, 3: 2, 4: 4, 5: 4, 6: 4, 7: 7}[j]), img_dev(0, 0, 1))
+            ("c", {0: 0, 1: 0, 6: 0, 2: 2, 3: 2, 4: 4, 5: 4, 7: 7}[j]), img_dev(0, 0, 1))
 
     pl.delay(1)
     for kinds in ((FLIP, FAR), (UP, DOWN)):
@@ -154,10 +154,11 @@
             await_all(("a", stream, 1, h))
             a_put(stream, FLIP_UP, h)
             a_put(stream, FLIP_DOWN, h)
+    across(1)
+    for h in range(CUT):
         for stream in (IMG, TXT):
             await_all(("a", stream, 6, h))
             a_put(stream, FLIP_FAR, h)
-    across(1)
     across(6)
     pl.delay(1)
     await_all(("a", IMG, 2))
@@ -222,7 +223,7 @@
     pl.delay(1)
     await_all(("c", 0))
     pl.delay(1)
-    units([(0, 0, span), (1, 0, span)])
+    units([(0, 0, span), (1, 0, span), (6, 0, span)])
     pl.delay(1)
     await_all(("c", 2))
     pl.delay(1)
@@ -240,7 +241,7 @@
     await_all(("a", IMG, 7))
     across(7)
     pl.delay(1)
-    units([(i, 0, span) for i in (4, 5, 6)] + [(i, span, pair) for i in (4, 5, 6)])
+    units([(i, 0, span) for i in (4, 5)] + [(i, span, pair) for i in (4, 5, 6)])
     pl.delay(1)
     await_all(("a", TXT, 7))
     await_all(("c", 7))
@@ -481,9 +482,9 @@
         return jnp.concatenate(out, axis=0)
 
     pl.delay(1)
-    gt_out[...] = finish(TXT).T.astype(gt_out.dtype)
-    pl.delay(1)
-    gi_out[...] = finish(IMG).astype(gi_out.dtype)
+    g_out[1] = finish(TXT).T.astype(BF16)
+    pl.delay(1)
+    g_out[0] = finish(IMG).astype(BF16)
     pl.delay(1)
     await_all(("three",))
     total = sc_three[0] + sc_three[1]
@@ -505,16 +506,15 @@
     rows, width = images.shape
     vmem = pl.BlockSpec(memory_space=pltpu.VMEM)
     dma = pltpu.SemaphoreType.DMA
-    gi, gt, loss, scale = pl.pallas_call(
+    g, loss, scale = pl.pallas_call(
         kernel,
         out_shape=(
-            jax.ShapeDtypeStruct(images.shape, images.dtype),
-            jax.ShapeDtypeStruct(texts.shape, texts.dtype),
+            pltpu.VMEM((2,) + images.shape, BF16),
             jax.ShapeDtypeStruct((1, 1), F32),
             jax.ShapeDtypeStruct((1, 1), F32),
         ),
         in_specs=[pl.BlockSpec(memory_space=pltpu.HBM)] * 3,
-        out_specs=(vmem,) * 4,
+        out_specs=(vmem,) * 3,
         scratch_shapes=[
             pltpu.VMEM((2 * COUNT * rows, width), BF16),
             pltpu.VMEM((width, 2 * COUNT * rows), BF16),
@@ -555,7 +555,7 @@
         compiler_params=pltpu.CompilerParams(
             collective_id=0, has_side_effects=True, vmem_limit_bytes=54880 * 1024),
     )(images, texts, log_scale.reshape(1, 1))
-    return gi, gt, loss.reshape(()), scale.reshape(())
+    return g[0], g[1], loss.reshape(()), scale.reshape(())
 
 
 def solution(mesh):

time: 50.4 us -> 49.7 us (0.986)
  local copies, waits for them, and re-layouts: 1.31 us -> 0.72 us
    unnamed x2 -> x0, local copies, waits for them, and re-layouts: 1.31 us -> none
    squeeze x0 -> x1, local copies, waits for them, and re-layouts: none -> 0.72 us  [body(): return (g[0], g[1], loss.reshape(()), scale.reshape(()))]
where the time goes in v7:
time: 49.7 us; the launch traced here: 49.5 us
  Pallas kernels  44 us (89%)
  between operations  4.81 us (10%)
  local copies, waits for them, and re-layouts  0.72 us (1%)
    pallas_call x1, Pallas kernels, body(): pl.pallas_call(kernel, out_shape=(pltpu.VMEM((2,) + images.shape, BF16),...  44 us

profile of v7, /device:TPU:1, one launch (start us, length us, event | category | flops | bytes accessed | tf_op | source)
XLA Modules:
  0.0 49.5 jit_solution(16985558334183103840)
XLA Ops:
  1.3 44.0 %shard_map.66 = (bf16[2,128,512]{2,1,0:T(8,128)(2,1)S(1)}, f32[1,1]{1,0:T(1,128)}, f32[1,1]{1,0:T(1,128)}) custom-call(bf16[128,512]{1,0:T(8,128)(2,1)} %images.1, bf16[128,512]{1,0:T(8,128)(2,1)} %texts.1, f32[1,1]{1,0:T(1,128)} %bitcast.7.log_scale), custom_call_target="tpu_custom_call" | custom-call | tf_op jit(solution)/shard_map/pallas_call | solution.py:509
  45.3 0.7 %slice_bitcast_fusion = (bf16[128,512]{1,0:T(8,128)(2,1)}, bf16[128,512]{1,0:T(8,128)(2,1)}) fusion(bf16[2,128,512]{2,1,0:T(8,128)(2,1)S(1)} %get-tuple-element.7), kind=kLoop, calls=%fused_computation | loop fusion | bytes 524288 | tf_op jit(solution)/shard_map/squeeze | solution.py:558

commit v8 on v7

--- a/solution.py
+++ b/solution.py
@@ -418,33 +418,33 @@
         give(stream, j, h, total)
 
     pl.delay(1)
-    weigh(6)
-    weigh(7)
+    weigh(4)
+    weigh(5)
+    pl.delay(1)
+    gi_blocks(4)
+    for j in (6, 7, 2, 3):
+        weigh(j)
+    gi_across(4)
     pl.delay(1)
     gi_blocks(6)
-    for j in (4, 5, 2, 3):
-        weigh(j)
-    gi_across(6)
-    pl.delay(1)
-    gi_blocks(4)
     for j in (0, 1):
         weigh(j)
     weigh_own()
-    gi_across(4)
+    gi_across(6)
     pl.delay(1)
     gt_half(1)
     scalar_one()
     scalar_send()
     pl.delay(1)
-    send(TXT, 7, 4, 5)
+    pair_sum(4)
+    pair_sum(5)
+    send(IMG, 4, 5)
+    pl.delay(1)
+    send(TXT, 4, 5, 7)
     pl.delay(1)
     pair_sum(6)
     pair_sum(7)
     send(IMG, 7)
-    pl.delay(1)
-    for j in (4, 5):
-        pair_sum(j)
-        send(IMG, j)
     pl.delay(1)
     gi_blocks(2)
     gi_across(2)

time: 49.7 us -> 49.5 us (level)
  no operation moved by 1% of the time
where the time goes in v8:
time: 49.5 us; the launch traced here: 49.3 us
  Pallas kernels  43.8 us (88%)
  between operations  4.81 us (10%)
  local copies, waits for them, and re-layouts  0.72 us (1%)
    pallas_call x1, Pallas kernels, body(): pl.pallas_call(kernel, out_shape=(pltpu.VMEM((2,) + images.shape, BF16),...  43.8 us

profile of v8, /device:TPU:1, one launch (start us, length us, event | category | flops | bytes accessed | tf_op | source)
XLA Modules:
  0.0 49.3 jit_solution(6564403397204199718)
XLA Ops:
  1.3 43.8 %shard_map.66 = (bf16[2,128,512]{2,1,0:T(8,128)(2,1)S(1)}, f32[1,1]{1,0:T(1,128)}, f32[1,1]{1,0:T(1,128)}) custom-call(bf16[128,512]{1,0:T(8,128)(2,1)} %images.1, bf16[128,512]{1,0:T(8,128)(2,1)} %texts.1, f32[1,1]{1,0:T(1,128)} %bitcast.7.log_scale), custom_call_target="tpu_custom_call" | custom-call | tf_op jit(solution)/shard_map/pallas_call | solution.py:509
  45.1 0.7 %slice_bitcast_fusion = (bf16[128,512]{1,0:T(8,128)(2,1)}, bf16[128,512]{1,0:T(8,128)(2,1)}) fusion(bf16[2,128,512]{2,1,0:T(8,128)(2,1)S(1)} %get-tuple-element.7), kind=kLoop, calls=%fused_computation | loop fusion | bytes 524288 | tf_op jit(solution)/shard_map/squeeze | solution.py:558

commit v9 on v8

--- a/solution.py
+++ b/solution.py
@@ -463,8 +463,8 @@
     pl.delay(1)
     for h in range(PART):
         send_on(TXT, 6, (7,), h)
+        send_on(IMG, 6, (7,), h)
         send_on(TXT, 1, (4, 5), h)
-        send_on(IMG, 6, (7,), h)
         if h == 0:
             pair_sum(0)
             pair_sum(1)

time: 49.5 us -> 49.5 us (level)
  no operation moved by 1% of the time
where the time goes in v9:
time: 49.5 us; the launch traced here: 49.3 us
  Pallas kernels  43.8 us (88%)
  between operations  4.81 us (10%)
  local copies, waits for them, and re-layouts  0.72 us (1%)
    pallas_call x1, Pallas kernels, body(): pl.pallas_call(kernel, out_shape=(pltpu.VMEM((2,) + images.shape, BF16),...  43.8 us

profile of v9, /device:TPU:1, one launch (start us, length us, event | category | flops | bytes accessed | tf_op | source)
XLA Modules:
  0.0 49.3 jit_solution(11657219763205573777)
XLA Ops:
  1.3 43.8 %shard_map.66 = (bf16[2,128,512]{2,1,0:T(8,128)(2,1)S(1)}, f32[1,1]{1,0:T(1,128)}, f32[1,1]{1,0:T(1,128)}) custom-call(bf16[128,512]{1,0:T(8,128)(2,1)} %images.1, bf16[128,512]{1,0:T(8,128)(2,1)} %texts.1, f32[1,1]{1,0:T(1,128)} %bitcast.7.log_scale), custom_call_target="tpu_custom_call" | custom-call | tf_op jit(solution)/shard_map/pallas_call | solution.py:509
  45.1 0.7 %slice_bitcast_fusion = (bf16[128,512]{1,0:T(8,128)(2,1)}, bf16[128,512]{1,0:T(8,128)(2,1)}) fusion(bf16[2,128,512]{2,1,0:T(8,128)(2,1)S(1)} %get-tuple-element.7), kind=kLoop, calls=%fused_computation | loop fusion | bytes 524288 | tf_op jit(solution)/shard_map/squeeze | solution.py:558
